TPU v7x, 256 devices: a whole 4x4x8 slice. The times are simulated.
256 devices in a mesh: group: 8 (over z), mp: 32 (over y, x, core).
Axes of the slice: x: 4, y: 4, z: 8, core: 2. Of those that a mesh axis runs over, the one named last changes fastest.
Arguments:
- option_latent_states: bfloat16 [2048, 8192], P('group', 'mp'), may hold values from -6 to 6
- mixer_scaling_factor: bfloat16 [1, 8192], P(None, 'mp'), may hold values from 0.099609375 to 1.8984375
- question_mapping_matrix: bfloat16 [8192, 8192], P(None, 'mp'), may hold values from -0.0625 to 0.0625
- lookup_content_matrix: bfloat16 [8192, 2048], P(None, 'mp'), may hold values from -0.0625 to 0.0625
- final_mapping_matrix: bfloat16 [8192, 8192], P('mp'), may hold values from -0.125 to 0.125
- payoff_readout_vector: bfloat16 [8192], P('mp'), may hold values from -0.0625 to 0.0625
- shared_trie_memo: bfloat16 [2, 512, 128, 1024], P(None, ('group', 'mp')), may hold values from -100 to 100
- option_route_pages: int32 [128, 32], P('group'), may hold values from 0 to 63, as said below
- option_page_tally: int32 [128], P('group'), may hold values from 1 to 32, as said below
- option_token_span: int32 [128], P('group'), may hold values from 1 to 16
- retained_pages: int32 [512], P(('group', 'mp')), may hold values from 0 to 1
- growth_place_mapping: int32 [768], P(('group', 'mp')), may hold values from 0 to 15, as said below
Outputs:
- scored_rows: bfloat16 [2048, 8192], P('group', 'mp')
- rewards: float32 [128], P('group')
- expanded: bfloat16 [2, 768, 128, 1024], P(None, ('group', 'mp'))
Inputs may be any that keep to these rules, and one draw needn't show every extreme that they name: `option_route_pages`: the t-th listed block of a candidate is one of t * 2 to (t + 1) * 2 - 1; entries at or past option_page_tally are not read. `option_page_tally`: among the 16 candidates of each group index one lists all 32 blocks. `growth_place_mapping`: for every mp index, every survivor of every group index fills some slot.
All inputs are finite; a program needn't handle non-finite values.
Results may differ from a plain program's by a relative error of at most 0.005.
The roundings to bfloat16 on the way count: a program that leaves them out, or rounds other values in their place, can miss the bound.
Values may be sent and summed in bfloat16 or wider, within the bound.
No kernel may reach another device: no remote copies, remote signals or barrier semaphores. Data moves between devices by JAX's collectives and lax.ppermute only.
A program may use at most 128 MiB of HBM per device.

v0:
```python
import jax
import jax.numpy as jnp
from jax import lax
from jax.experimental import pallas as pl
from jax.experimental.pallas import tpu as pltpu
from jax.sharding import Mesh
from jax.sharding import PartitionSpec as P


D = 8192
KVH = 8
HD = 128
BLK = 128
STEP = 16
ROWS = 256
HALF = 128
EXTRA = 16
TALL = ROWS + EXTRA
GROUPS = 8
PART = ROWS // GROUPS
SIDE = 4
SLOTS = 3
CHIPS = 16
FEAT = 256
MP = ("mp_0", "mp_1", "mp_2")
CHIP = ("mp_0", "mp_1")
GROUP_MP = ("group", "mp_0", "mp_1", "mp_2")


epsilon = 1e-06
masked_value = -1e30
LOG2E = 1.4426950408889634
MIB = 1024 * 1024
ATTEND_ROOM = 40
DEAL_ROOM = 60

VM = pl.BlockSpec(memory_space=pltpu.VMEM)
SM = pl.BlockSpec(memory_space=pltpu.SMEM)
PLACE = pl.BlockSpec(memory_space=pl.ANY)


def call(kernel, outs, operands, specs, flops=1 << 22, scratch=(), room=8):
    size = sum(a.size * a.dtype.itemsize for a in outs) * 2
    return pl.pallas_call(
        kernel,
        out_shape=tuple(outs),
        in_specs=specs,
        out_specs=(VM,) * len(outs),
        scratch_shapes=scratch,
        compiler_params=pltpu.CompilerParams(vmem_limit_bytes=room * MIB),
        cost_estimate=pl.CostEstimate(flops=flops, bytes_accessed=size, transcendentals=0),
    )(*operands)


def shaped(*shape, dtype=jnp.bfloat16):
    return jax.ShapeDtypeStruct(shape, dtype)


def wrap(at, size):
    return lax.rem(at + size, size)


def deal_pool_kernel(kept_ref, memo_ref, keys_ref, values_ref, kept_out):
    for entry in range(2):
        second = kept_ref[entry] == 1
        for half in range(2):
            kept_out[entry, half] = jnp.where(second, memo_ref[half, 1], memo_ref[half, 0])
    for chip in range(CHIPS):
        lanes = slice(chip // 2 * HD, (chip // 2 + 1) * HD)
        keys_ref[chip] = memo_ref[0, :, :, lanes]
        values_ref[chip] = memo_ref[1, :, :, lanes]


def deal_pool(kept, memo):
    return call(
        deal_pool_kernel,
        [
            shaped(CHIPS, 2, BLK, HD),
            shaped(CHIPS, 2, BLK, HD),
            shaped(2, 2, BLK, KVH * HD),
        ],
        (kept, memo),
        [SM, VM],
        room=DEAL_ROOM,
    )


def ahead(core, j):
    return jnp.where(core == 0, (j + 1) % 4, 7 - j)


def deal_rows_kernel(where_ref, in_ref, extra_ref, keep_ref, give_ref):
    core, group = where_ref[2], where_ref[3]
    for j in range(4):
        keep_ref[j] = in_ref[lax.rem(group + ahead(core, j), GROUPS)]
        give_ref[j * PART : (j + 1) * PART, :] = in_ref[lax.rem(group + ahead(1 - core, j), GROUPS)]
    give_ref[HALF:, :] = extra_ref[...]


def deal_rows(where, states, extra):
    return call(
        deal_rows_kernel,
        [shaped(4, PART, FEAT), shaped(HALF + EXTRA, FEAT)],
        (where, states.reshape(GROUPS, PART, FEAT), extra),
        [SM, VM, VM],
    )


def pair_rows_kernel(keep_ref, got_ref, *out_refs):
    for j, out_ref in enumerate(out_refs):
        out_ref[0] = keep_ref[j]
        out_ref[1] = got_ref[j * PART : (j + 1) * PART, :]


def pair_rows(keep, got):
    return call(pair_rows_kernel, [shaped(2, PART, FEAT)] * 4, (keep, got), [VM, VM])


def bundle_rows_kernel(extra_ref, got_ref, *refs):
    out_ref = refs[4]
    for j in range(4):
        out_ref[:, j * PART : (j + 1) * PART, :] = refs[j][...]
    out_ref[0, HALF:, :] = extra_ref[...]
    out_ref[1, HALF:, :] = got_ref[HALF:, :]


def bundle_rows(extra, got, received):
    return call(
        bundle_rows_kernel, [shaped(2, HALF + EXTRA, FEAT)], (extra, got, *received), [VM] * 6
    )[0]


def place_kernel(label_ref, in_ref, out_ref):
    out_ref[...] = in_ref[...].reshape(out_ref.shape)


def place(labels, survivors):
    return pl.pallas_call(
        place_kernel,
        out_shape=shaped(2, SLOTS, BLK, KVH * HD),
        grid_spec=pltpu.PrefetchScalarGridSpec(
            num_scalar_prefetch=1,
            grid=(SLOTS, 2),
            in_specs=[
                pl.BlockSpec((1, 1, BLK, KVH * HD), lambda e, h, label: (label[e], h, 0, 0))
            ],
            out_specs=pl.BlockSpec((1, 1, BLK, KVH * HD), lambda e, h, label: (h, e, 0, 0)),
        ),
        compiler_params=pltpu.CompilerParams(vmem_limit_bytes=60 * MIB),
        cost_estimate=pl.CostEstimate(flops=1 << 22, bytes_accessed=3 << 20, transcendentals=0),
        name="place",
    )(labels, survivors)


def project_kernel(where_ref, *refs):
    blocks, (wq_hbm, wkv_hbm, q_ref, kv_ref, pay_ref) = refs[:8], refs[8:13]
    pieces, (wq_ref, wkv_ref, scaled, squares, sems) = refs[13:21], refs[21:]
    copies = [
        pltpu.make_async_copy(source, target, sems.at[n])
        for n, (source, target) in enumerate(
            zip((*blocks, wkv_hbm, wq_hbm), (*pieces, wkv_ref, wq_ref))
        )
    ]
    for copy in copies:
        copy.start()
    y, x, core, group = where_ref[0], where_ref[1], where_ref[2], where_ref[3]
    squares[...] = jnp.zeros_like(squares)
    for other in range(2):
        holder = core if other == 0 else 1 - core
        spots = []
        for j in range(4):
            source = wrap(group - ahead(holder, j), GROUPS)
            spots.append(pl.ds(pl.multiple_of(source * PART, PART), PART))
        for first in range(SIDE):
            copies[other * 4 + first].wait()
            piece_ref = pieces[other * 4 + first]
            for second in range(SIDE):
                back_y = jnp.where(holder == 0, first, second)
                back_x = jnp.where(holder == 0, second, first)
                chip = wrap(y - back_y, SIDE) * SIDE + wrap(x - back_x, SIDE)
                for b in range(2):
                    block = chip * 2 + (holder if b == 0 else 1 - holder)
                    place = pl.ds(pl.multiple_of(block * FEAT, FEAT), FEAT)
                    extra = piece_ref[second, b, HALF:, :].astype(jnp.float32)
                    gain = extra[0:1]
                    pay_ref[0:1, place] = extra[1:2]
                    for j in range(4):
                        rows = spots[j]
                        piece = piece_ref[second, b, j * PART : (j + 1) * PART, :]
                        wide = piece.astype(jnp.float32)
                        scaled[rows, place] = (wide * gain).astype(jnp.bfloat16)
                        square = wide * wide
                        squares[rows, :] += square[:, :HD] + square[:, HD:]
    copies[8].wait()
    copies[9].wait()
    step = 1024

    def multiply(i, sums):
        q_sum, kv_sum = sums
        at = pl.ds(pl.multiple_of(i * step, step), step)
        part = scaled[:, at]
        q_sum += jnp.dot(part, wq_ref[at, :], preferred_element_type=jnp.float32)
        kv_sum += lax.dot_general(
            part, wkv_ref[:, at], (((1,), (1,)), ((), ())), preferred_element_type=jnp.float32
        )
        return q_sum, kv_sum

    q_sum, kv_sum = lax.fori_loop(
        0,
        D // step,
        multiply,
        (jnp.zeros((ROWS, FEAT), jnp.float32), jnp.zeros((ROWS, 64), jnp.float32)),
    )
    total = squares[...]
    down = lax.rsqrt(jnp.sum(total, axis=1, keepdims=True) / D + epsilon)
    q_ref[...] = (q_sum * down).astype(jnp.bfloat16)
    kv_ref[...] = (kv_sum * down).T.astype(jnp.bfloat16)


def project(where, pieces, wq, wkv):
    return pl.pallas_call(
        project_kernel,
        out_shape=(
            jax.ShapeDtypeStruct((ROWS, FEAT), jnp.bfloat16),
            jax.ShapeDtypeStruct((64, ROWS), jnp.bfloat16),
            jax.ShapeDtypeStruct((1, D), jnp.float32),
        ),
        in_specs=[SM] + [PLACE] * 10,
        out_specs=(VM, VM, VM),
        scratch_shapes=[pltpu.VMEM(p.shape, p.dtype) for p in (*pieces, wq, wkv)]
        + [
            pltpu.VMEM((ROWS, D), jnp.bfloat16),
            pltpu.VMEM((ROWS, HD), jnp.float32),
            pltpu.SemaphoreType.DMA((10,)),
        ],
        compiler_params=pltpu.CompilerParams(vmem_limit_bytes=60 * MIB),
        cost_estimate=pl.CostEstimate(
            flops=2 * ROWS * D * 320, bytes_accessed=10 << 20, transcendentals=0
        ),
        name="project",
    )(where, *pieces, wq, wkv)


def attend_kernel(
    where_ref,
    q_ref,
    near_keys,
    far_keys,
    near_values,
    far_values,
    choice_ref,
    own_ref,
    a_same,
    a_cross,
    b_same,
    b_cross,
    keep_ref,
    give_ref,
    queries,
    scores,
    tops,
    masses,
    sums,
    near_ref,
    far_ref,
    sems,
):
    copies = []
    for n, source in enumerate((near_keys, far_keys, near_values, far_values)):
        target = (near_ref, far_ref)[n % 2]
        copies.append(pltpu.make_async_copy(source, target.at[n // 2], sems.at[n]))
        copies[n].start()
    score_scale = HD ** (-0.5) * LOG2E
    rows = 2 * ROWS
    core, odd = where_ref[2], lax.rem(where_ref[1], 2)
    queries[:ROWS, :] = q_ref[:, :HD]
    queries[ROWS:, :] = q_ref[:, HD:]
    low, even = core == 0, odd == 0

    def put_together(same, cross):
        return jnp.concatenate(
            [jnp.where(low, same, cross), jnp.where(low, cross, same)], axis=0
        )

    first = put_together(a_same[...], a_cross[...])
    second = put_together(b_same[...], b_cross[...])
    fresh_keys = jnp.where(even, first, second)
    fresh_values = jnp.where(even, second, first)
    own_mask = own_ref[...] > 0.5
    own_mask = jnp.concatenate([own_mask, own_mask], axis=0)
    own_score = (
        jnp.dot(queries[...], fresh_keys, preferred_element_type=jnp.float32) * score_scale
    )
    own_score = jnp.where(own_mask, own_score, masked_value)
    tops[...] = jnp.maximum(own_score[:, :HD], own_score[:, HD:])

    def chosen(which):
        spread = jnp.broadcast_to(choice_ref[which][:, None, :], (ROWS // STEP, STEP, HD))
        spread = spread.reshape(ROWS, HD)
        return jnp.concatenate([spread, spread], axis=0)

    def score(i, _):
        for other, source in ((0, near_ref), (1, far_ref)):
            choice = chosen(i * 2 + lax.rem(core + other, 2))
            keys = source[0, i].reshape(2 * BLK, HD)
            both = lax.dot_general(
                queries[...], keys, (((1,), (1,)), ((), ())), preferred_element_type=jnp.float32
            )
            one = jnp.where(choice > 0.5, both[:, BLK:], both[:, :BLK]) * score_scale
            one = jnp.where(choice > 1.5, masked_value, one)
            scores[i * 2 + other] = one
            tops[...] = jnp.maximum(tops[...], one)
        return 0

    copies[0].wait()
    copies[1].wait()
    lax.fori_loop(0, CHIPS, score, 0)
    top = jnp.max(tops[...], axis=1, keepdims=True)
    tops[...] = jnp.broadcast_to(top, (rows, HD))
    own_mass = jnp.where(own_mask, jnp.exp2(own_score - top), 0.0)
    masses[...] = own_mass[:, :HD] + own_mass[:, HD:]
    sums[...] = lax.dot_general(
        own_mass.astype(jnp.bfloat16),
        fresh_values,
        (((1,), (1,)), ((), ())),
        preferred_element_type=jnp.float32,
    )

    def weigh(i, _):
        for other, source in ((0, near_ref), (1, far_ref)):
            choice = chosen(i * 2 + lax.rem(core + other, 2))
            mass = jnp.exp2(scores[i * 2 + other] - tops[...])
            masses[...] += mass
            weights = jnp.concatenate(
                [jnp.where(choice > 0.5, 0.0, mass), jnp.where(choice > 0.5, mass, 0.0)], axis=1
            ).astype(jnp.bfloat16)
            values = source[1, i].reshape(2 * BLK, HD)
            sums[...] += jnp.dot(weights, values, preferred_element_type=jnp.float32)
        return 0

    copies[2].wait()
    copies[3].wait()
    lax.fori_loop(0, CHIPS, weigh, 0)
    attended = sums[...] / jnp.sum(masses[...], axis=1, keepdims=True)
    sums[...] = attended
    for mine, out_ref in ((core, keep_ref), (1 - core, give_ref)):
        for head in range(2):
            at = pl.multiple_of(head * ROWS + mine * HALF, HALF)
            out_ref[:, head * HD : (head + 1) * HD] = sums[pl.ds(at, HALF), :].astype(jnp.bfloat16)


def attend(where, queries, cached, choice, own_mask, fresh):
    return pl.pallas_call(
        attend_kernel,
        out_shape=(shaped(HALF, FEAT), shaped(HALF, FEAT)),
        in_specs=[SM, VM] + [PLACE] * 4 + [VM] * 6,
        out_specs=(VM, VM),
        scratch_shapes=[
            pltpu.VMEM((2 * ROWS, HD), jnp.bfloat16),
            pltpu.VMEM((2 * CHIPS, 2 * ROWS, HD), jnp.float32),
            pltpu.VMEM((2 * ROWS, HD), jnp.float32),
            pltpu.VMEM((2 * ROWS, HD), jnp.float32),
            pltpu.VMEM((2 * ROWS, HD), jnp.float32),
            pltpu.VMEM((2, CHIPS, 2, BLK, HD), jnp.bfloat16),
            pltpu.VMEM((2, CHIPS, 2, BLK, HD), jnp.bfloat16),
            pltpu.SemaphoreType.DMA((4,)),
        ],
        compiler_params=pltpu.CompilerParams(vmem_limit_bytes=ATTEND_ROOM * MIB),
        cost_estimate=pl.CostEstimate(
            flops=8 * ROWS * 8192 * 256, bytes_accessed=5 << 20, transcendentals=ROWS * 8192
        ),
        name="attend",
    )(where, queries, *cached, choice, own_mask, *fresh)


def in_terms(row):
    terms = []
    for _ in range(3):
        term = row.astype(jnp.bfloat16)
        row = row - term.astype(jnp.float32)
        terms.append(term.astype(jnp.float32))
    terms.append(jnp.zeros((EXTRA - 3, row.shape[1]), jnp.float32))
    return jnp.concatenate(terms, axis=0).astype(jnp.bfloat16)


def of_terms(block):
    return (block[0:1] + block[1:2]) + block[2:3]


def four(parts):
    return (parts[0] + parts[2]) + (parts[1] + parts[3])


def finish_kernel(where_ref, near_ref, far_ref, wo_ref, wo_far, pay_ref, last_ref, *refs):
    outs, reward = refs[:4], refs[4]
    y, x, core = where_ref[0], where_ref[1], where_ref[2]
    reward[...] = jnp.zeros_like(reward)
    for first in range(SIDE):
        out_ref = outs[first]

        def multiply(second, _, first=first, out_ref=out_ref):
            ahead_y = jnp.where(core == 0, second, first)
            ahead_x = jnp.where(core == 0, first, second)
            chip = lax.rem(y + ahead_y, SIDE) * SIDE + lax.rem(x + ahead_x, SIDE)
            place = pl.ds(pl.multiple_of(chip * 2 * FEAT, 2 * FEAT), 2 * FEAT)
            part = jnp.dot(near_ref[...], wo_ref[:, place], preferred_element_type=jnp.float32)
            part += jnp.dot(far_ref[...], wo_far[:, place], preferred_element_type=jnp.float32)
            out_ref[second, :HALF, :] = part[:, :FEAT].astype(jnp.bfloat16)
            out_ref[second, HALF:ROWS, :] = part[:, FEAT:].astype(jnp.bfloat16)
            paid = part * pay_ref[0:1, place]
            paid = paid[:, :FEAT] + paid[:, FEAT:]
            reward[...] += paid[:, :HD] + paid[:, HD:]
            return 0

        lax.fori_loop(0, SIDE, multiply, 0, unroll=2)
    last = jnp.where(core == 0, last_ref[:, :HALF], last_ref[:, HALF:])
    row = jnp.sum(reward[...].T, axis=0, keepdims=True) * last
    terms = in_terms(jnp.concatenate([row, jnp.zeros_like(row)], axis=1))
    for out_ref in outs:
        for second in range(SIDE):
            out_ref[second, ROWS:, :] = terms


def finish(where, near, far, wo, wo_far, pay, last_row):
    return call(
        finish_kernel,
        [shaped(SIDE, TALL, FEAT)] * SIDE,
        (where, near, far, wo, wo_far, pay, last_row),
        [SM] + [VM] * 6,
        flops=2 * ROWS * 512 * 4096,
        scratch=[pltpu.VMEM((HALF, HD), jnp.float32)],
        room=20,
    )


def add_first_kernel(*refs):
    ins, outs = refs[:4], refs[4:]
    for k, out_ref in enumerate(outs):
        for at in range(0, ROWS, 64):
            rows = slice(at, at + 64)
            total = four([ref[k, rows, :].astype(jnp.float32) for ref in ins])
            out_ref[rows, :] = total.astype(jnp.bfloat16)
        extra = four([ref[k, ROWS:, :].astype(jnp.float32) for ref in ins])
        out_ref[ROWS:, :] = in_terms(of_terms(extra))


def add_first(parts):
    return call(add_first_kernel, [shaped(TALL, FEAT)] * 4, parts, [VM] * 4)


def add_second_kernel(where_ref, live_ref, *refs):
    ins, keep_ref, give_ref, total_ref = refs[:4], refs[4], refs[5], refs[6]
    core = where_ref[2]
    live = live_ref[pl.ds(pl.multiple_of(core * HALF, HALF), HALF), :]
    live = jnp.concatenate([live, live], axis=1)
    for column in range(2):
        rows = slice(column * HALF, (column + 1) * HALF)
        total = four([ref[rows, :].astype(jnp.float32) for ref in ins])
        total_ref[column] = (total * live).astype(jnp.bfloat16)
    keep_ref[:HALF, :] = total_ref[core]
    give_ref[:HALF, :] = total_ref[1 - core]
    extra = four([ref[ROWS:, :].astype(jnp.float32) for ref in ins])
    terms = in_terms(of_terms(extra))
    keep_ref[HALF:, :] = terms
    give_ref[HALF:, :] = terms


def add_second(where, live, parts):
    return call(
        add_second_kernel,
        [shaped(HALF + EXTRA, FEAT)] * 2,
        (where, live, *parts),
        [SM] + [VM] * 5,
        scratch=[pltpu.VMEM((2, HALF, FEAT), jnp.bfloat16)],
    )


def settle_kernel(where_ref, keep_ref, got_ref, out_ref, reward_ref):
    low = where_ref[2] == 0
    upper = jnp.where(low, keep_ref[...], got_ref[...])
    lower = jnp.where(low, got_ref[...], keep_ref[...])
    out_ref[:HALF, :] = upper[:HALF]
    out_ref[HALF:, :] = lower[:HALF]
    reward_ref[:, :HALF] = of_terms(upper[HALF:].astype(jnp.float32))[:, :HALF]
    reward_ref[:, HALF:] = of_terms(lower[HALF:].astype(jnp.float32))[:, :HALF]


def settle(where, keep, got):
    return call(
        settle_kernel,
        [shaped(ROWS, FEAT), shaped(1, ROWS, dtype=jnp.float32)],
        (where, keep, got),
        [SM, VM, VM],
    )


def turned(x, first, by):
    moves = []
    for y in range(SIDE):
        for x_at in range(SIDE):
            for core in range(2):
                along_x = (core == 0) == first
                to_y = y if along_x else (y + by) % SIDE
                to_x = (x_at + by) % SIDE if along_x else x_at
                moves.append(
                    ((y * SIDE + x_at) * 2 + core, (to_y * SIDE + to_x) * 2 + core)
                )
    return lax.ppermute(x, MP, moves)


def over_groups(x, j):
    moves = []
    for group in range(GROUPS):
        for core in range(2):
            by = (j + 1) % 4 if core == 0 else 7 - j
            moves.append((group * 2 + core, (group + by) % GROUPS * 2 + core))
    return lax.ppermute(x, ("group", "mp_2"), moves)


def exchange(x, axis):
    return lax.all_to_all(x, axis, split_axis=0, concat_axis=0, tiled=True)


def swapped(x, axis, bit):
    size = lax.axis_size(axis)
    return lax.ppermute(x, axis, [(i, i ^ bit) for i in range(size)])


def local(
    option_latent_states,
    mixer_scaling_factor,
    question_mapping_matrix,
    lookup_content_matrix,
    final_mapping_matrix,
    payoff_readout_vector,
    shared_trie_memo,
    option_route_pages,
    option_page_tally,
    option_token_span,
    retained_pages,
    growth_place_mapping,
):
    where = jnp.stack([lax.axis_index(a) for a in (*MP, "group")]).astype(jnp.int32)
    cand_here = ROWS // STEP

    keys, values, survivors = deal_pool(retained_pages, shared_trie_memo)
    survivors = lax.all_gather(survivors, "group", axis=0, tiled=True)
    near_keys = exchange(keys, CHIP)
    far_keys = swapped(near_keys, "mp_2", 1)

    extra = jnp.concatenate(
        [
            mixer_scaling_factor,
            payoff_readout_vector[None],
            jnp.zeros((EXTRA - 2, FEAT), jnp.bfloat16),
        ],
        axis=0,
    )
    kept_rows, given_rows = deal_rows(where, option_latent_states, extra)
    got_rows = swapped(given_rows, "mp_2", 1)
    received = [over_groups(x, j) for j, x in enumerate(pair_rows(kept_rows, got_rows))]
    mine = bundle_rows(extra, got_rows, received)

    mine = [mine] + [turned(mine, True, k) for k in (1, 2, 3)]
    mine = jnp.stack(mine)
    pieces = [mine] + [turned(mine, False, k) for k in (1, 2, 3)]
    pieces = pieces + [swapped(p, "mp_2", 1) for p in pieces]
    near_values = exchange(values, CHIP)
    far_values = swapped(near_values, "mp_2", 1)
    wo_far = swapped(final_mapping_matrix, "mp_2", 1)

    queries, pair_part, pay = project(
        where, pieces, question_mapping_matrix, lookup_content_matrix.T
    )

    fresh = []
    for swap in (0, 1):
        moves = []
        for h in range(KVH):
            for value in (0, 1):
                moves.append((h + KVH * value, 2 * h + (value ^ swap)))
        same = lax.ppermute(pair_part, CHIP, moves)
        fresh += [same, swapped(same, "mp_2", 1)]

    table = option_route_pages.shape[1]
    index = jnp.arange(table, dtype=jnp.int32)[:, None]
    choice = jnp.where(
        index < option_page_tally[None, :], option_route_pages.T - 2 * index, 2
    ).astype(jnp.float32)
    choice = jnp.broadcast_to(choice[:, :, None], (table, cand_here, HD))
    row = jnp.arange(ROWS, dtype=jnp.int32)
    span_row = jnp.broadcast_to(option_token_span[:, None], (cand_here, STEP)).reshape(ROWS)
    own_mask = (
        (row[:, None] // STEP == row[None, :] // STEP)
        & (row[None, :] <= row[:, None])
        & (row[None, :] % STEP < span_row[:, None])
    ).astype(jnp.float32)
    kept_heads, given_heads = attend(
        where,
        queries,
        (near_keys, far_keys, near_values, far_values),
        choice,
        own_mask,
        fresh,
    )

    last_row = (row % STEP == span_row - 1).astype(jnp.float32)[None, :]
    parts = finish(
        where,
        kept_heads,
        swapped(given_heads, "mp_2", 1),
        final_mapping_matrix,
        wo_far,
        pay,
        last_row,
    )
    parts = [parts[0]] + [turned(parts[k], True, k) for k in (1, 2, 3)]
    sums = add_first(parts)
    sums = [sums[0]] + [turned(sums[k], False, k) for k in (1, 2, 3)]
    live_rows = (row % STEP < span_row).astype(jnp.float32)
    live_rows = jnp.broadcast_to(live_rows[:, None], (ROWS, HD))
    kept_sums, given_sums = add_second(where, live_rows, sums)
    scored_rows, rewards = settle(where, kept_sums, swapped(given_sums, "mp_2", 1))
    rewards = jnp.sum(rewards.reshape(cand_here, STEP), axis=1)

    expanded = place(growth_place_mapping, survivors)
    return (scored_rows, rewards, expanded)


def solution(mesh):
    split = Mesh(
        mesh.devices.reshape(mesh.shape["group"], 4, 4, 2), ("group", "mp_0", "mp_1", "mp_2")
    )
    in_specs = (
        P("group", MP),
        P(None, MP),
        P(None, MP),
        P(None, MP),
        P(MP, None),
        P(MP),
        P(None, GROUP_MP, None, None),
        P("group", None),
        P("group"),
        P("group"),
        P(GROUP_MP),
        P(GROUP_MP),
    )
    out_specs = (P("group", MP), P("group"), P(None, GROUP_MP, None, None))

    return jax.shard_map(local, mesh=split, in_specs=in_specs, out_specs=out_specs, check_vma=False)
```

profile of v0, /device:TPU:1, one launch (start us, length us, event | category | flops | bytes accessed | tf_op | source)
XLA Modules:
  0.0 167.0 jit_solution(11078235610993371559)
XLA Ops:
  7.3 3.1 %shard_map.142 = (bf16[16,2,128,128]{3,2,1,0:T(8,128)(2,1)}, bf16[16,2,128,128]{3,2,1,0:T(8,128)(2,1)}, bf16[2,2,128,1024]{3,2,1,0:T(8,128)(2,1)}) custom-call(s32[2]{0:T(128)} %kept_ref.1, bf16[2,2,128,1024]{3,2,1,0:T(8,128)(2,1)} %memo_ref.1), custom_call_target="tpu_custom_call" | custom-call | flops 4194304 | bytes 6291456 | tf_op jit(solution)/shard_map/pallas_call | solution.py:44
  10.3 3.3 %collective-permute-start.22 = (bf16[256,8192]{1,0:T(8,128)(2,1)}, bf16[256,8192]{1,0:T(8,128)(2,1)}, u32[]{:S(2)}, u32[]{:S(2)}) collective-permute-start(bf16[256,8192]{1,0:T(8,128)(2,1)} %wo_ref.1), channel_id=1, source_target_pairs={{0,1},{1,0},{2,3},{3,2},{4,5},{5,4},{6,7},{7,6},{8,9},{9,8},{10,11... | collective-permute-start | bytes 12582920 | tf_op jit(solution)/shard_map/ppermute | solution.py:526
  13.6 5.0 %all-to-all-start = ((bf16[16,2,128,128]{3,2,1,0:T(8,128)(2,1)}), bf16[16,2,128,128]{3,2,1,0:T(8,128)(2,1)S(1)}, u32[]{:S(2)}, u32[]{:S(2)}) async-start(bf16[16,2,128,128]{3,2,1,0:T(8,128)(2,1)} %get-tuple-element.36), calls=%async_computation | async-start | bytes 2097152 | tf_op jit(solution)/shard_map/all_to_all | solution.py:521
  20.9 5.7 %collective-permute-start.1 = (bf16[2,32,256]{2,1,0:T(8,128)(2,1)S(1)}, bf16[2,32,256]{2,1,0:T(8,128)(2,1)S(1)}, u32[]{:S(2)}, u32[]{:S(2)}) collective-permute-start(bf16[2,32,256]{2,1,0:T(8,128)(2,1)S(1)} %get-tuple-element.31), channel_id=1, source_target_pairs={{0,32},{1,225},{32,64},{33,1},{64,96},{65,33},{96,128},{97,65},{12... | collective-permute-start | bytes 98312 | tf_op jit(solution)/shard_map/ppermute | solution.py:517
  28.2 6.4 %collective-permute-start.4 = (bf16[2,32,256]{2,1,0:T(8,128)(2,1)S(1)}, bf16[2,32,256]{2,1,0:T(8,128)(2,1)S(1)}, u32[]{:S(2)}, u32[]{:S(2)}) collective-permute-start(bf16[2,32,256]{2,1,0:T(8,128)(2,1)S(1)} %get-tuple-element.34), channel_id=1, source_target_pairs={{0,0},{1,129},{32,32},{33,161},{64,64},{65,193},{96,96},{97,225},{... | collective-permute-start | bytes 98312 | tf_op jit(solution)/shard_map/ppermute | solution.py:517
  34.6 3.3 %collective-permute-done.4.refs_3_ = bf16[2,32,256]{2,1,0:T(8,128)(2,1)S(1)} collective-permute-done((bf16[2,32,256]{2,1,0:T(8,128)(2,1)S(1)}, bf16[2,32,256]{2,1,0:T(8,128)(2,1)S(1)}, u32[]{:S(2)}, u32[]{:S(2)}) %collective-permute-start.4) | collective-permute-done | bytes 32800 | tf_op jit(solution)/shard_map/ppermute | solution.py:517
  39.6 2.4 %collective-permute-start.6 = (bf16[2,144,256]{2,1,0:T(8,128)(2,1)S(1)}, bf16[2,144,256]{2,1,0:T(8,128)(2,1)S(1)}, u32[]{:S(2)}, u32[]{:S(2)}) collective-permute-start(bf16[2,144,256]{2,1,0:T(8,128)(2,1)S(1)} %shard_map.141), channel_id=1, source_target_pairs={{0,4},{1,17},{2,6},{3,19},{4,0},{5,21},{6,2},{7,23},{8,12},{9,25},... | collective-permute-start | bytes 442376 | tf_op jit(solution)/shard_map/ppermute | solution.py:508
  43.7 2.4 %collective-permute-done.6 = bf16[2,144,256]{2,1,0:T(8,128)(2,1)S(1)} collective-permute-done((bf16[2,144,256]{2,1,0:T(8,128)(2,1)S(1)}, bf16[2,144,256]{2,1,0:T(8,128)(2,1)S(1)}, u32[]{:S(2)}, u32[]{:S(2)}) %collective-permute-start.6) | collective-permute-done | bytes 147488 | tf_op jit(solution)/shard_map/ppermute | solution.py:508
  47.7 6.0 %all-to-all-start.1 = ((bf16[16,2,128,128]{3,2,1,0:T(8,128)(2,1)}), bf16[16,2,128,128]{3,2,1,0:T(8,128)(2,1)S(1)}, u32[]{:S(2)}, u32[]{:S(2)}) async-start(bf16[16,2,128,128]{3,2,1,0:T(8,128)(2,1)} %get-tuple-element.37), calls=%async_computation.1 | async-start | bytes 2097152 | tf_op jit(solution)/shard_map/all_to_all | solution.py:521
  53.7 2.9 %collective-permute-start.9 = (bf16[4,2,144,256]{3,2,1,0:T(8,128)(2,1)S(1)}, bf16[4,2,144,256]{3,2,1,0:T(8,128)(2,1)}, u32[]{:S(2)}, u32[]{:S(2)}) collective-permute-start(bf16[4,2,144,256]{3,2,1,0:T(8,128)(2,1)S(1)} %pad_maximum_fusion.refs_0_), channel_id=1, source_target_pairs={{0,16},{1,5},{2,18},{3,7},{4,20},{5,1},{6,22},{7,3},{8,24},{9,13},... | collective-permute-start | bytes 1769480 | tf_op jit(solution)/shard_map/ppermute | solution.py:508
  58.0 17.9 %collective-permute-done.9.refs_2_ = bf16[4,2,144,256]{3,2,1,0:T(8,128)(2,1)} collective-permute-done((bf16[4,2,144,256]{3,2,1,0:T(8,128)(2,1)S(1)}, bf16[4,2,144,256]{3,2,1,0:T(8,128)(2,1)}, u32[]{:S(2)}, u32[]{:S(2)}) %collective-permute-start.9) | collective-permute-done | bytes 589856 | tf_op jit(solution)/shard_map/ppermute | solution.py:508
  75.9 3.8 %collective-permute-done.10.refs_3_ = bf16[4,2,144,256]{3,2,1,0:T(8,128)(2,1)} collective-permute-done((bf16[4,2,144,256]{3,2,1,0:T(8,128)(2,1)S(1)}, bf16[4,2,144,256]{3,2,1,0:T(8,128)(2,1)}, u32[]{:S(2)}, u32[]{:S(2)}) %collective-permute-start.10) | collective-permute-done | bytes 589856 | tf_op jit(solution)/shard_map/ppermute | solution.py:508
  82.0 9.4 %project.1 = (bf16[256,256]{1,0:T(8,128)(2,1)}, bf16[64,256]{1,0:T(8,128)(2,1)}, f32[1,8192]{1,0:T(1,128)}) custom-call(s32[4]{0:T(128)} %copy-done.3, bf16[4,2,144,256]{3,2,1,0:T(8,128)(2,1)} %copy-done.6, bf16[4,2,144,256]{3,2,1,0:T(8,128)(2,1)} %collective-permute-done.8.refs_1_, bf16[4,2,144,256]{3,2,1,0:T(8,128)(2,1)} %collective-permute-done.9.refs_2_, ...), custom_call_target="tpu_custom_call" | custom-call | flops 1342177280 | bytes 10485760 | tf_op jit(solution)/shard_map/project/pallas_call | solution.py:221
  92.8 2.9 %collective-permute-start.19 = (bf16[64,256]{1,0:T(8,128)(2,1)}, bf16[64,256]{1,0:T(8,128)(2,1)S(1)}, u32[]{:S(2)}, u32[]{:S(2)}) collective-permute-start(bf16[64,256]{1,0:T(8,128)(2,1)} %get-tuple-element.38), channel_id=1, source_target_pairs={{0,2},{16,0},{2,6},{18,4},{4,10},{20,8},{6,14},{22,12},{8,18},{24,... | collective-permute-start | bytes 98312 | tf_op jit(solution)/shard_map/ppermute | solution.py:582
  103.5 11.3 %attend.1 = (bf16[128,256]{1,0:T(8,128)(2,1)S(1)}, bf16[128,256]{1,0:T(8,128)(2,1)S(1)}) custom-call(s32[4]{0:T(128)S(1)} %copy-done.4, bf16[256,256]{1,0:T(8,128)(2,1)S(1)} %copy-done.5, bf16[16,2,128,128]{3,2,1,0:T(8,128)(2,1)S(1)} %all-to-all-done.near_keys, bf16[16,2,128,128]{3,2,1,0:T(8,128)(2,1)S(1)} %collective-permute-done.15.far_keys, ...), custom_call_target="tpu_custom_call" | custom-call | flops 4294967296 | bytes 5242880 | tf_op jit(solution)/shard_map/attend/pallas_call | solution.py:353
  116.2 4.9 %shard_map.143 = (bf16[4,272,256]{2,1,0:T(8,128)(2,1)S(1)}, bf16[4,272,256]{2,1,0:T(8,128)(2,1)S(1)}, bf16[4,272,256]{2,1,0:T(8,128)(2,1)S(1)}, bf16[4,272,256]{2,1,0:T(8,128)(2,1)S(1)}) custom-call(s32[4]{0:T(128)S(1)} %copy-done.4, bf16[128,256]{1,0:T(8,128)(2,1)S(1)} %get-tuple-element.39.near_ref, bf16[128,256]{1,0:T(8,128)(2,1)S(1)} %collective-permute-done.21.far_ref, ...), custom_call_target="tpu_custom_call" | custom-call | flops 1073741824 | bytes 4456448 | tf_op jit(solution)/shard_map/pallas_call | solution.py:44
  121.1 2.5 %collective-permute-start.23 = (bf16[4,272,256]{2,1,0:T(8,128)(2,1)S(1)}, bf16[4,272,256]{2,1,0:T(8,128)(2,1)S(1)}, u32[]{:S(2)}, u32[]{:S(2)}) collective-permute-start(bf16[4,272,256]{2,1,0:T(8,128)(2,1)S(1)} %get-tuple-element.43), channel_id=1, source_target_pairs={{0,2},{1,9},{2,4},{3,11},{4,6},{5,13},{6,0},{7,15},{8,10},{9,17},{... | collective-permute-start | bytes 1671176 | tf_op jit(solution)/shard_map/ppermute | solution.py:508
  123.7 2.7 %collective-permute-start.24 = (bf16[4,272,256]{2,1,0:T(8,128)(2,1)S(1)}, bf16[4,272,256]{2,1,0:T(8,128)(2,1)S(1)}, u32[]{:S(2)}, u32[]{:S(2)}) collective-permute-start(bf16[4,272,256]{2,1,0:T(8,128)(2,1)S(1)} %get-tuple-element.44), channel_id=1, source_target_pairs={{0,4},{1,17},{2,6},{3,19},{4,0},{5,21},{6,2},{7,23},{8,12},{9,25},... | collective-permute-start | bytes 1671176 | tf_op jit(solution)/shard_map/ppermute | solution.py:508
  126.3 6.0 %collective-permute-done.23.refs_1_ = bf16[4,272,256]{2,1,0:T(8,128)(2,1)S(1)} collective-permute-done((bf16[4,272,256]{2,1,0:T(8,128)(2,1)S(1)}, bf16[4,272,256]{2,1,0:T(8,128)(2,1)S(1)}, u32[]{:S(2)}, u32[]{:S(2)}) %collective-permute-start.23) | collective-permute-done | bytes 557088 | tf_op jit(solution)/shard_map/ppermute | solution.py:508
  132.4 7.1 %collective-permute-done.24.refs_2_ = bf16[4,272,256]{2,1,0:T(8,128)(2,1)S(1)} collective-permute-done((bf16[4,272,256]{2,1,0:T(8,128)(2,1)S(1)}, bf16[4,272,256]{2,1,0:T(8,128)(2,1)S(1)}, u32[]{:S(2)}, u32[]{:S(2)}) %collective-permute-start.24) | collective-permute-done | bytes 557088 | tf_op jit(solution)/shard_map/ppermute | solution.py:508
  141.3 2.2 %collective-permute-start.27 = (bf16[272,256]{1,0:T(8,128)(2,1)S(1)}, bf16[272,256]{1,0:T(8,128)(2,1)S(1)}, u32[]{:S(2)}, u32[]{:S(2)}) collective-permute-start(bf16[272,256]{1,0:T(8,128)(2,1)S(1)} %get-tuple-element.48), channel_id=1, source_target_pairs={{0,16},{1,5},{2,18},{3,7},{4,20},{5,1},{6,22},{7,3},{8,24},{9,13},... | collective-permute-start | bytes 417800 | tf_op jit(solution)/shard_map/ppermute | solution.py:508
  145.0 2.7 %collective-permute-done.27.refs_2_ = bf16[272,256]{1,0:T(8,128)(2,1)S(1)} collective-permute-done((bf16[272,256]{1,0:T(8,128)(2,1)S(1)}, bf16[272,256]{1,0:T(8,128)(2,1)S(1)}, u32[]{:S(2)}, u32[]{:S(2)}) %collective-permute-start.27) | collective-permute-done | bytes 139296 | tf_op jit(solution)/shard_map/ppermute | solution.py:508
  148.5 2.5 %collective-permute-start.29 = (bf16[144,256]{1,0:T(8,128)(2,1)S(1)}, bf16[144,256]{1,0:T(8,128)(2,1)S(1)}, u32[]{:S(2)}, u32[]{:S(2)}) collective-permute-start(bf16[144,256]{1,0:T(8,128)(2,1)S(1)} %get-tuple-element.51), channel_id=1, source_target_pairs={{0,1},{1,0},{2,3},{3,2},{4,5},{5,4},{6,7},{7,6},{8,9},{9,8},{10,11... | collective-permute-start | bytes 221192 | tf_op jit(solution)/shard_map/ppermute | solution.py:526
  155.0 5.2 %place.1 = bf16[2,3,128,1024]{3,2,1,0:T(8,128)(2,1)} custom-call(s32[3]{0:T(128)} %label_ref.1, bf16[16,2,128,1024]{3,2,1,0:T(8,128)(2,1)} %all-gather.2.cloned.1.call-done.in_ref), custom_call_target="tpu_custom_call" | custom-call | flops 4194304 | bytes 3145728 | tf_op jit(solution)/shard_map/place/pallas_call | solution.py:138
  (106 shorter events, 31.2 us)
Async XLA Ops:
  7.2 147.7 %all-gather.2.cloned.1.call-start = ((), (), s32[]{:S(2)}) async-start(), calls=%async_computation.2 | async-start | bytes 9437184 | tf_op jit(solution)/shard_map/all_gather | solution.py:547
  10.3 105.9 %collective-permute-start.22 = (bf16[256,8192]{1,0:T(8,128)(2,1)}, bf16[256,8192]{1,0:T(8,128)(2,1)}, u32[]{:S(2)}, u32[]{:S(2)}) collective-permute-start(bf16[256,8192]{1,0:T(8,128)(2,1)} %wo_ref.1), channel_id=1, source_target_pairs={{0,1},{1,0},{2,3},{3,2},{4,5},{5,4},{6,7},{7,6},{8,9},{9,8},{10,11... | collective-permute-start | bytes 12582920 | tf_op jit(solution)/shard_map/ppermute | solution.py:526
  13.6 34.1 %all-to-all-start = ((bf16[16,2,128,128]{3,2,1,0:T(8,128)(2,1)}), bf16[16,2,128,128]{3,2,1,0:T(8,128)(2,1)S(1)}, u32[]{:S(2)}, u32[]{:S(2)}) async-start(bf16[16,2,128,128]{3,2,1,0:T(8,128)(2,1)} %get-tuple-element.36), calls=%async_computation | async-start | bytes 2097152 | tf_op jit(solution)/shard_map/all_to_all | solution.py:521
  20.9 13.7 %collective-permute-start.1 = (bf16[2,32,256]{2,1,0:T(8,128)(2,1)S(1)}, bf16[2,32,256]{2,1,0:T(8,128)(2,1)S(1)}, u32[]{:S(2)}, u32[]{:S(2)}) collective-permute-start(bf16[2,32,256]{2,1,0:T(8,128)(2,1)S(1)} %get-tuple-element.31), channel_id=1, source_target_pairs={{0,32},{1,225},{32,64},{33,1},{64,96},{65,33},{96,128},{97,65},{12... | collective-permute-start | bytes 98312 | tf_op jit(solution)/shard_map/ppermute | solution.py:517
  26.6 8.0 %collective-permute-start.2 = (bf16[2,32,256]{2,1,0:T(8,128)(2,1)S(1)}, bf16[2,32,256]{2,1,0:T(8,128)(2,1)S(1)}, u32[]{:S(2)}, u32[]{:S(2)}) collective-permute-start(bf16[2,32,256]{2,1,0:T(8,128)(2,1)S(1)} %get-tuple-element.32), channel_id=1, source_target_pairs={{0,64},{1,193},{32,96},{33,225},{64,128},{65,1},{96,160},{97,33},{... | collective-permute-start | bytes 98312 | tf_op jit(solution)/shard_map/ppermute | solution.py:517
  27.7 6.9 %collective-permute-start.3 = (bf16[2,32,256]{2,1,0:T(8,128)(2,1)S(1)}, bf16[2,32,256]{2,1,0:T(8,128)(2,1)S(1)}, u32[]{:S(2)}, u32[]{:S(2)}) collective-permute-start(bf16[2,32,256]{2,1,0:T(8,128)(2,1)S(1)} %get-tuple-element.33), channel_id=1, source_target_pairs={{0,96},{1,161},{32,128},{33,193},{64,160},{65,225},{96,192},{97,1}... | collective-permute-start | bytes 98312 | tf_op jit(solution)/shard_map/ppermute | solution.py:517
  28.2 9.7 %collective-permute-start.4 = (bf16[2,32,256]{2,1,0:T(8,128)(2,1)S(1)}, bf16[2,32,256]{2,1,0:T(8,128)(2,1)S(1)}, u32[]{:S(2)}, u32[]{:S(2)}) collective-permute-start(bf16[2,32,256]{2,1,0:T(8,128)(2,1)S(1)} %get-tuple-element.34), channel_id=1, source_target_pairs={{0,0},{1,129},{32,32},{33,161},{64,64},{65,193},{96,96},{97,225},{... | collective-permute-start | bytes 98312 | tf_op jit(solution)/shard_map/ppermute | solution.py:517
  37.9 5.8 %collective-permute-start.5 = (bf16[2,144,256]{2,1,0:T(8,128)(2,1)S(1)}, bf16[2,144,256]{2,1,0:T(8,128)(2,1)S(1)}, u32[]{:S(2)}, u32[]{:S(2)}) collective-permute-start(bf16[2,144,256]{2,1,0:T(8,128)(2,1)S(1)} %shard_map.141), channel_id=1, source_target_pairs={{0,2},{1,9},{2,4},{3,11},{4,6},{5,13},{6,0},{7,15},{8,10},{9,17},{... | collective-permute-start | bytes 442376 | tf_op jit(solution)/shard_map/ppermute | solution.py:508
  39.6 6.6 %collective-permute-start.6 = (bf16[2,144,256]{2,1,0:T(8,128)(2,1)S(1)}, bf16[2,144,256]{2,1,0:T(8,128)(2,1)S(1)}, u32[]{:S(2)}, u32[]{:S(2)}) collective-permute-start(bf16[2,144,256]{2,1,0:T(8,128)(2,1)S(1)} %shard_map.141), channel_id=1, source_target_pairs={{0,4},{1,17},{2,6},{3,19},{4,0},{5,21},{6,2},{7,23},{8,12},{9,25},... | collective-permute-start | bytes 442376 | tf_op jit(solution)/shard_map/ppermute | solution.py:508
  46.5 11.0 %collective-permute-start.8 = (bf16[4,2,144,256]{3,2,1,0:T(8,128)(2,1)S(1)}, bf16[4,2,144,256]{3,2,1,0:T(8,128)(2,1)}, u32[]{:S(2)}, u32[]{:S(2)}) collective-permute-start(bf16[4,2,144,256]{3,2,1,0:T(8,128)(2,1)S(1)} %pad_maximum_fusion.refs_0_), channel_id=1, source_target_pairs={{0,8},{1,3},{2,10},{3,5},{4,12},{5,7},{6,14},{7,1},{8,16},{9,11},{... | collective-permute-start | bytes 1769480 | tf_op jit(solution)/shard_map/ppermute | solution.py:508
  47.7 33.3 %all-to-all-start.1 = ((bf16[16,2,128,128]{3,2,1,0:T(8,128)(2,1)}), bf16[16,2,128,128]{3,2,1,0:T(8,128)(2,1)S(1)}, u32[]{:S(2)}, u32[]{:S(2)}) async-start(bf16[16,2,128,128]{3,2,1,0:T(8,128)(2,1)} %get-tuple-element.37), calls=%async_computation.1 | async-start | bytes 2097152 | tf_op jit(solution)/shard_map/all_to_all | solution.py:521
  53.7 22.2 %collective-permute-start.9 = (bf16[4,2,144,256]{3,2,1,0:T(8,128)(2,1)S(1)}, bf16[4,2,144,256]{3,2,1,0:T(8,128)(2,1)}, u32[]{:S(2)}, u32[]{:S(2)}) collective-permute-start(bf16[4,2,144,256]{3,2,1,0:T(8,128)(2,1)S(1)} %pad_maximum_fusion.refs_0_), channel_id=1, source_target_pairs={{0,16},{1,5},{2,18},{3,7},{4,20},{5,1},{6,22},{7,3},{8,24},{9,13},... | collective-permute-start | bytes 1769480 | tf_op jit(solution)/shard_map/ppermute | solution.py:508
  56.6 23.1 %collective-permute-start.10 = (bf16[4,2,144,256]{3,2,1,0:T(8,128)(2,1)S(1)}, bf16[4,2,144,256]{3,2,1,0:T(8,128)(2,1)}, u32[]{:S(2)}, u32[]{:S(2)}) collective-permute-start(bf16[4,2,144,256]{3,2,1,0:T(8,128)(2,1)S(1)} %pad_maximum_fusion.refs_0_), channel_id=1, source_target_pairs={{0,24},{1,7},{2,26},{3,1},{4,28},{5,3},{6,30},{7,5},{8,0},{9,15},{... | collective-permute-start | bytes 1769480 | tf_op jit(solution)/shard_map/ppermute | solution.py:508
  57.5 22.5 %collective-permute-start.11 = (bf16[4,2,144,256]{3,2,1,0:T(8,128)(2,1)S(1)}, bf16[4,2,144,256]{3,2,1,0:T(8,128)(2,1)S(1)}, u32[]{:S(2)}, u32[]{:S(2)}) collective-permute-start(bf16[4,2,144,256]{3,2,1,0:T(8,128)(2,1)S(1)} %pad_maximum_fusion.refs_0_), channel_id=1, source_target_pairs={{0,1},{1,0},{2,3},{3,2},{4,5},{5,4},{6,7},{7,6},{8,9},{9,8},{10,11... | collective-permute-start | bytes 1769480 | tf_op jit(solution)/shard_map/ppermute | solution.py:526
  57.5 23.5 %collective-permute-start.12 = (bf16[4,2,144,256]{3,2,1,0:T(8,128)(2,1)}, bf16[4,2,144,256]{3,2,1,0:T(8,128)(2,1)}, u32[]{:S(2)}, u32[]{:S(2)}) collective-permute-start(bf16[4,2,144,256]{3,2,1,0:T(8,128)(2,1)} %collective-permute-done.8.refs_1_), channel_id=1, source_target_pairs={{0,1},{1,0},{2,3},{3,2},{4,5},{5,4},{6,7},{7,6},{8,9},{9,8},{10,11... | collective-permute-start | bytes 1769480 | tf_op jit(solution)/shard_map/ppermute | solution.py:526
  75.9 5.8 %collective-permute-start.13 = (bf16[4,2,144,256]{3,2,1,0:T(8,128)(2,1)}, bf16[4,2,144,256]{3,2,1,0:T(8,128)(2,1)}, u32[]{:S(2)}, u32[]{:S(2)}) collective-permute-start(bf16[4,2,144,256]{3,2,1,0:T(8,128)(2,1)} %collective-permute-done.9.refs_2_), channel_id=1, source_target_pairs={{0,1},{1,0},{2,3},{3,2},{4,5},{5,4},{6,7},{7,6},{8,9},{9,8},{10,11... | collective-permute-start | bytes 1769480 | tf_op jit(solution)/shard_map/ppermute | solution.py:526
  80.8 20.3 %collective-permute-start.15 = (bf16[16,2,128,128]{3,2,1,0:T(8,128)(2,1)S(1)}, bf16[16,2,128,128]{3,2,1,0:T(8,128)(2,1)S(1)}, u32[]{:S(2)}, u32[]{:S(2)}) collective-permute-start(bf16[16,2,128,128]{3,2,1,0:T(8,128)(2,1)S(1)} %all-to-all-done.near_keys), channel_id=1, source_target_pairs={{0,1},{1,0},{2,3},{3,2},{4,5},{5,4},{6,7},{7,6},{8,9},{9,8},{10,11... | collective-permute-start | bytes 3145736 | tf_op jit(solution)/shard_map/ppermute | solution.py:526
  81.0 20.1 %collective-permute-start.16 = (bf16[16,2,128,128]{3,2,1,0:T(8,128)(2,1)S(1)}, bf16[16,2,128,128]{3,2,1,0:T(8,128)(2,1)}, u32[]{:S(2)}, u32[]{:S(2)}) collective-permute-start(bf16[16,2,128,128]{3,2,1,0:T(8,128)(2,1)S(1)} %all-to-all-done.1.near_values), channel_id=1, source_target_pairs={{0,1},{1,0},{2,3},{3,2},{4,5},{5,4},{6,7},{7,6},{8,9},{9,8},{10,11... | collective-permute-start | bytes 3145736 | tf_op jit(solution)/shard_map/ppermute | solution.py:526
  92.8 5.9 %collective-permute-start.19 = (bf16[64,256]{1,0:T(8,128)(2,1)}, bf16[64,256]{1,0:T(8,128)(2,1)S(1)}, u32[]{:S(2)}, u32[]{:S(2)}) collective-permute-start(bf16[64,256]{1,0:T(8,128)(2,1)} %get-tuple-element.38), channel_id=1, source_target_pairs={{0,2},{16,0},{2,6},{18,4},{4,10},{20,8},{6,14},{22,12},{8,18},{24,... | collective-permute-start | bytes 98312 | tf_op jit(solution)/shard_map/ppermute | solution.py:582
  95.8 5.3 %collective-permute-start.18 = (bf16[64,256]{1,0:T(8,128)(2,1)S(1)}, bf16[64,256]{1,0:T(8,128)(2,1)S(1)}, u32[]{:S(2)}, u32[]{:S(2)}) collective-permute-start(bf16[64,256]{1,0:T(8,128)(2,1)S(1)} %collective-permute-done.17.a_same), channel_id=1, source_target_pairs={{0,1},{1,0},{2,3},{3,2},{4,5},{5,4},{6,7},{7,6},{8,9},{9,8},{10,11... | collective-permute-start | bytes 98312 | tf_op jit(solution)/shard_map/ppermute | solution.py:526
  121.1 11.3 %collective-permute-start.23 = (bf16[4,272,256]{2,1,0:T(8,128)(2,1)S(1)}, bf16[4,272,256]{2,1,0:T(8,128)(2,1)S(1)}, u32[]{:S(2)}, u32[]{:S(2)}) collective-permute-start(bf16[4,272,256]{2,1,0:T(8,128)(2,1)S(1)} %get-tuple-element.43), channel_id=1, source_target_pairs={{0,2},{1,9},{2,4},{3,11},{4,6},{5,13},{6,0},{7,15},{8,10},{9,17},{... | collective-permute-start | bytes 1671176 | tf_op jit(solution)/shard_map/ppermute | solution.py:508
  123.7 15.9 %collective-permute-start.24 = (bf16[4,272,256]{2,1,0:T(8,128)(2,1)S(1)}, bf16[4,272,256]{2,1,0:T(8,128)(2,1)S(1)}, u32[]{:S(2)}, u32[]{:S(2)}) collective-permute-start(bf16[4,272,256]{2,1,0:T(8,128)(2,1)S(1)} %get-tuple-element.44), channel_id=1, source_target_pairs={{0,4},{1,17},{2,6},{3,19},{4,0},{5,21},{6,2},{7,23},{8,12},{9,25},... | collective-permute-start | bytes 1671176 | tf_op jit(solution)/shard_map/ppermute | solution.py:508
  126.3 13.2 %collective-permute-start.25 = (bf16[4,272,256]{2,1,0:T(8,128)(2,1)S(1)}, bf16[4,272,256]{2,1,0:T(8,128)(2,1)S(1)}, u32[]{:S(2)}, u32[]{:S(2)}) collective-permute-start(bf16[4,272,256]{2,1,0:T(8,128)(2,1)S(1)} %get-tuple-element.45), channel_id=1, source_target_pairs={{0,6},{1,25},{2,0},{3,27},{4,2},{5,29},{6,4},{7,31},{8,14},{9,1},{... | collective-permute-start | bytes 1671176 | tf_op jit(solution)/shard_map/ppermute | solution.py:508
  141.3 6.4 %collective-permute-start.27 = (bf16[272,256]{1,0:T(8,128)(2,1)S(1)}, bf16[272,256]{1,0:T(8,128)(2,1)S(1)}, u32[]{:S(2)}, u32[]{:S(2)}) collective-permute-start(bf16[272,256]{1,0:T(8,128)(2,1)S(1)} %get-tuple-element.48), channel_id=1, source_target_pairs={{0,16},{1,5},{2,18},{3,7},{4,20},{5,1},{6,22},{7,3},{8,24},{9,13},... | collective-permute-start | bytes 417800 | tf_op jit(solution)/shard_map/ppermute | solution.py:508
  (23 other events, 308.1 us)
Sparse Core Ops, SparseCore 0:
  10.5 99.7 all-gather.1
where the time goes:
time: 169 us; the launch traced here: 167 us
  starting transfers between devices  59.3 us (35%)
  waiting for transfers between devices  50 us (30%)
  Pallas kernels  36.6 us (22%)
  between operations  14.3 us (8%)
  local copies, waits for them, and re-layouts  5 us (3%)
  other arithmetic  1.75 us (1%)
    ppermute x12, waiting for transfers between devices, turned(): return lax.ppermute(x, MP, moves)  41.5 us
    ppermute x12, starting transfers between devices, turned(): return lax.ppermute(x, MP, moves)  19.9 us
    ppermute x4, starting transfers between devices, over_groups(): return lax.ppermute(x, ('group', 'mp_2'), moves)  13.7 us
    pallas_call x1, Pallas kernels, attend(): pl.pallas_call(attend_kernel, out_shape=(shaped(HALF, FEAT), shaped(HALF,...  11.3 us
    all_to_all x2, starting transfers between devices, exchange(): return lax.all_to_all(x, axis, split_axis=0, concat_axis=0, tiled=True)  11 us
    pallas_call x8, Pallas kernels, call(): pl.pallas_call(kernel, out_shape=tuple(outs), in_specs=specs, out_specs=(...  10.7 us
    ppermute x12, starting transfers between devices, swapped(): return lax.ppermute(x, axis, [(i, i ^ bit) for i in range(size)])  10.3 us
    pallas_call x1, Pallas kernels, project(): pl.pallas_call(project_kernel, out_shape=(jax.ShapeDtypeStruct((ROWS, FEA...  9.38 us
  transfers between devices with their start and end apart: 33, of which 15 were waited for; matrix products, arithmetic and copies ran while one was open for 3% of the time, Pallas kernels for 17%

commit v1 on v0

--- a/solution.py
+++ b/solution.py
@@ -31,12 +31,12 @@
 masked_value = -1e30
 LOG2E = 1.4426950408889634
 MIB = 1024 * 1024
-ATTEND_ROOM = 40
+ATTEND_ROOM = 24
 DEAL_ROOM = 60
 
 VM = pl.BlockSpec(memory_space=pltpu.VMEM)
 SM = pl.BlockSpec(memory_space=pltpu.SMEM)
-PLACE = pl.BlockSpec(memory_space=pl.ANY)
+FAR = pl.BlockSpec(memory_space=pltpu.HBM)
 
 
 def call(kernel, outs, operands, specs, flops=1 << 22, scratch=(), room=8):
@@ -89,20 +89,19 @@
     return jnp.where(core == 0, (j + 1) % 4, 7 - j)
 
 
-def deal_rows_kernel(where_ref, in_ref, extra_ref, keep_ref, give_ref):
+def deal_rows_kernel(where_ref, in_ref, keep_ref, give_ref):
     core, group = where_ref[2], where_ref[3]
     for j in range(4):
         keep_ref[j] = in_ref[lax.rem(group + ahead(core, j), GROUPS)]
         give_ref[j * PART : (j + 1) * PART, :] = in_ref[lax.rem(group + ahead(1 - core, j), GROUPS)]
-    give_ref[HALF:, :] = extra_ref[...]
-
-
-def deal_rows(where, states, extra):
+
+
+def deal_rows(where, states):
     return call(
         deal_rows_kernel,
-        [shaped(4, PART, FEAT), shaped(HALF + EXTRA, FEAT)],
-        (where, states.reshape(GROUPS, PART, FEAT), extra),
-        [SM, VM, VM],
+        [shaped(4, PART, FEAT), shaped(HALF, FEAT)],
+        (where, states.reshape(GROUPS, PART, FEAT)),
+        [SM, VM],
     )
 
 
@@ -121,13 +120,53 @@
     for j in range(4):
         out_ref[:, j * PART : (j + 1) * PART, :] = refs[j][...]
     out_ref[0, HALF:, :] = extra_ref[...]
-    out_ref[1, HALF:, :] = got_ref[HALF:, :]
+    out_ref[1, HALF:, :] = got_ref[...]
 
 
 def bundle_rows(extra, got, received):
     return call(
         bundle_rows_kernel, [shaped(2, HALF + EXTRA, FEAT)], (extra, got, *received), [VM] * 6
     )[0]
+
+
+def marks_kernel(pages_ref, tally_ref, span_ref, choice_ref, own_ref, last_ref, live_ref):
+    cands, table = pages_ref.shape
+
+    def mark(t, _):
+        for c in range(cands):
+            value = jnp.where(t < tally_ref[c], pages_ref[c, t] - 2 * t, 2)
+            choice_ref[t, c : c + 1, :] = jnp.full((1, HD), value, jnp.int32).astype(jnp.float32)
+        return 0
+
+    lax.fori_loop(0, table, mark, 0)
+    lane = lax.broadcasted_iota(jnp.int32, (STEP, ROWS), 1)
+    row = lax.broadcasted_iota(jnp.int32, (STEP, ROWS), 0)
+    flat = lane[0:1]
+    last = jnp.zeros((1, ROWS), jnp.float32)
+    for c in range(cands):
+        span = span_ref[c]
+        here = lane // STEP == c
+        own = here & (lane % STEP <= row) & (lane % STEP < span)
+        rows = slice(c * STEP, (c + 1) * STEP)
+        own_ref[rows, :] = own.astype(jnp.float32)
+        last = jnp.where((flat // STEP == c) & (flat % STEP == span - 1), 1.0, last)
+        live_ref[rows, :] = (row[:, :HD] < span).astype(jnp.float32)
+    last_ref[...] = last
+
+
+def marks(pages, tally, span):
+    cands, table = pages.shape
+    return call(
+        marks_kernel,
+        [
+            shaped(table, cands, HD, dtype=jnp.float32),
+            shaped(ROWS, ROWS, dtype=jnp.float32),
+            shaped(1, ROWS, dtype=jnp.float32),
+            shaped(ROWS, HD, dtype=jnp.float32),
+        ],
+        (pages, tally, span),
+        [SM] * 3,
+    )
 
 
 def place_kernel(label_ref, in_ref, out_ref):
@@ -225,7 +264,7 @@
             jax.ShapeDtypeStruct((64, ROWS), jnp.bfloat16),
             jax.ShapeDtypeStruct((1, D), jnp.float32),
         ),
-        in_specs=[SM] + [PLACE] * 10,
+        in_specs=[SM] + [FAR] * 10,
         out_specs=(VM, VM, VM),
         scratch_shapes=[pltpu.VMEM(p.shape, p.dtype) for p in (*pieces, wq, wkv)]
         + [
@@ -243,17 +282,15 @@
 
 def attend_kernel(
     where_ref,
-    q_ref,
+    q_hbm,
     near_keys,
     far_keys,
     near_values,
     far_values,
-    choice_ref,
-    own_ref,
-    a_same,
-    a_cross,
-    b_same,
-    b_cross,
+    choice_hbm,
+    own_hbm,
+    fresh_ref,
+    fresh_far,
     keep_ref,
     give_ref,
     queries,
@@ -263,29 +300,33 @@
     sums,
     near_ref,
     far_ref,
+    q_ref,
+    choice_ref,
+    own_ref,
     sems,
 ):
-    copies = []
-    for n, source in enumerate((near_keys, far_keys, near_values, far_values)):
-        target = (near_ref, far_ref)[n % 2]
-        copies.append(pltpu.make_async_copy(source, target.at[n // 2], sems.at[n]))
+    moves = [
+        (near_keys, near_ref.at[0]),
+        (far_keys, far_ref.at[0]),
+        (near_values, near_ref.at[1]),
+        (far_values, far_ref.at[1]),
+        (q_hbm, q_ref),
+        (own_hbm, own_ref),
+        (choice_hbm, choice_ref),
+    ]
+    copies = [pltpu.make_async_copy(*move, sems.at[n]) for n, move in enumerate(moves)]
+    for n in (4, 5, 6, 0, 1, 2, 3):
         copies[n].start()
+    copies[4].wait()
+    copies[5].wait()
     score_scale = HD ** (-0.5) * LOG2E
     rows = 2 * ROWS
-    core, odd = where_ref[2], lax.rem(where_ref[1], 2)
+    core = where_ref[2]
     queries[:ROWS, :] = q_ref[:, :HD]
     queries[ROWS:, :] = q_ref[:, HD:]
-    low, even = core == 0, odd == 0
-
-    def put_together(same, cross):
-        return jnp.concatenate(
-            [jnp.where(low, same, cross), jnp.where(low, cross, same)], axis=0
-        )
-
-    first = put_together(a_same[...], a_cross[...])
-    second = put_together(b_same[...], b_cross[...])
-    fresh_keys = jnp.where(even, first, second)
-    fresh_values = jnp.where(even, second, first)
+    low = core == 0
+    fresh_keys = jnp.where(low, fresh_ref[...], fresh_far[...])
+    fresh_values = jnp.where(low, fresh_far[...], fresh_ref[...])
     own_mask = own_ref[...] > 0.5
     own_mask = jnp.concatenate([own_mask, own_mask], axis=0)
     own_score = (
@@ -312,9 +353,10 @@
             tops[...] = jnp.maximum(tops[...], one)
         return 0
 
+    copies[6].wait()
     copies[0].wait()
     copies[1].wait()
-    lax.fori_loop(0, CHIPS, score, 0)
+    lax.fori_loop(0, CHIPS, score, 0, unroll=2)
     top = jnp.max(tops[...], axis=1, keepdims=True)
     tops[...] = jnp.broadcast_to(top, (rows, HD))
     own_mass = jnp.where(own_mask, jnp.exp2(own_score - top), 0.0)
@@ -340,7 +382,7 @@
 
     copies[2].wait()
     copies[3].wait()
-    lax.fori_loop(0, CHIPS, weigh, 0)
+    lax.fori_loop(0, CHIPS, weigh, 0, unroll=2)
     attended = sums[...] / jnp.sum(masses[...], axis=1, keepdims=True)
     sums[...] = attended
     for mine, out_ref in ((core, keep_ref), (1 - core, give_ref)):
@@ -353,7 +395,7 @@
     return pl.pallas_call(
         attend_kernel,
         out_shape=(shaped(HALF, FEAT), shaped(HALF, FEAT)),
-        in_specs=[SM, VM] + [PLACE] * 4 + [VM] * 6,
+        in_specs=[SM] + [FAR] * 7 + [VM] * 2,
         out_specs=(VM, VM),
         scratch_shapes=[
             pltpu.VMEM((2 * ROWS, HD), jnp.bfloat16),
@@ -363,7 +405,10 @@
             pltpu.VMEM((2 * ROWS, HD), jnp.float32),
             pltpu.VMEM((2, CHIPS, 2, BLK, HD), jnp.bfloat16),
             pltpu.VMEM((2, CHIPS, 2, BLK, HD), jnp.bfloat16),
-            pltpu.SemaphoreType.DMA((4,)),
+            pltpu.VMEM((ROWS, FEAT), jnp.bfloat16),
+            pltpu.VMEM(choice.shape, jnp.float32),
+            pltpu.VMEM(own_mask.shape, jnp.float32),
+            pltpu.SemaphoreType.DMA((7,)),
         ],
         compiler_params=pltpu.CompilerParams(vmem_limit_bytes=ATTEND_ROOM * MIB),
         cost_estimate=pl.CostEstimate(
@@ -481,14 +526,17 @@
     lower = jnp.where(low, got_ref[...], keep_ref[...])
     out_ref[:HALF, :] = upper[:HALF]
     out_ref[HALF:, :] = lower[:HALF]
-    reward_ref[:, :HALF] = of_terms(upper[HALF:].astype(jnp.float32))[:, :HALF]
-    reward_ref[:, HALF:] = of_terms(lower[HALF:].astype(jnp.float32))[:, :HALF]
+    terms = jnp.concatenate([upper[HALF:, :HALF], lower[HALF:, :HALF]], axis=1)
+    row = lax.broadcasted_iota(jnp.int32, (ROWS, HD), 0)
+    lane = lax.broadcasted_iota(jnp.int32, (ROWS, HD), 1)
+    member = (row // STEP == lane).astype(jnp.bfloat16)
+    reward_ref[...] = of_terms(jnp.dot(terms, member, preferred_element_type=jnp.float32))
 
 
 def settle(where, keep, got):
     return call(
         settle_kernel,
-        [shaped(ROWS, FEAT), shaped(1, ROWS, dtype=jnp.float32)],
+        [shaped(ROWS, FEAT), shaped(1, HD, dtype=jnp.float32)],
         (where, keep, got),
         [SM, VM, VM],
     )
@@ -548,6 +596,11 @@
     near_keys = exchange(keys, CHIP)
     far_keys = swapped(near_keys, "mp_2", 1)
 
+    kept_rows, given_rows = deal_rows(where, option_latent_states)
+    got_rows = swapped(given_rows, "mp_2", 1)
+    received = []
+    for j, x in enumerate(pair_rows(kept_rows, got_rows)):
+        received.append(over_groups(x, j))
     extra = jnp.concatenate(
         [
             mixer_scaling_factor,
@@ -556,55 +609,51 @@
         ],
         axis=0,
     )
-    kept_rows, given_rows = deal_rows(where, option_latent_states, extra)
-    got_rows = swapped(given_rows, "mp_2", 1)
-    received = [over_groups(x, j) for j, x in enumerate(pair_rows(kept_rows, got_rows))]
-    mine = bundle_rows(extra, got_rows, received)
+    got_extra = swapped(extra, "mp_2", 1)
+    mine = bundle_rows(extra, got_extra, received)
 
     mine = [mine] + [turned(mine, True, k) for k in (1, 2, 3)]
     mine = jnp.stack(mine)
-    pieces = [mine] + [turned(mine, False, k) for k in (1, 2, 3)]
+    pieces = [mine]
+    for k in (1, 2, 3):
+        pieces.append(turned(mine, False, k))
     pieces = pieces + [swapped(p, "mp_2", 1) for p in pieces]
     near_values = exchange(values, CHIP)
     far_values = swapped(near_values, "mp_2", 1)
     wo_far = swapped(final_mapping_matrix, "mp_2", 1)
 
+    choice, own_mask, last_row, live_rows = marks(
+        option_route_pages, option_page_tally, option_token_span
+    )
     queries, pair_part, pay = project(
-        where, pieces, question_mapping_matrix, lookup_content_matrix.T
-    )
-
-    fresh = []
-    for swap in (0, 1):
-        moves = []
-        for h in range(KVH):
-            for value in (0, 1):
-                moves.append((h + KVH * value, 2 * h + (value ^ swap)))
-        same = lax.ppermute(pair_part, CHIP, moves)
-        fresh += [same, swapped(same, "mp_2", 1)]
-
-    table = option_route_pages.shape[1]
-    index = jnp.arange(table, dtype=jnp.int32)[:, None]
-    choice = jnp.where(
-        index < option_page_tally[None, :], option_route_pages.T - 2 * index, 2
-    ).astype(jnp.float32)
-    choice = jnp.broadcast_to(choice[:, :, None], (table, cand_here, HD))
-    row = jnp.arange(ROWS, dtype=jnp.int32)
-    span_row = jnp.broadcast_to(option_token_span[:, None], (cand_here, STEP)).reshape(ROWS)
-    own_mask = (
-        (row[:, None] // STEP == row[None, :] // STEP)
-        & (row[None, :] <= row[:, None])
-        & (row[None, :] % STEP < span_row[:, None])
-    ).astype(jnp.float32)
+        where,
+        pieces,
+        question_mapping_matrix,
+        lookup_content_matrix.T,
+    )
+
+    partner = swapped(pair_part, "mp_2", 1)
+    low = where[2] == 0
+    both = jnp.concatenate(
+        [jnp.where(low, pair_part, partner), jnp.where(low, partner, pair_part)], axis=0
+    )
+    moves = []
+    for h in range(KVH):
+        for value in (0, 1):
+            for odd in (0, 1):
+                moves.append(((h + KVH * value) * 2 + odd, (2 * h + odd) * 2 + value))
+    fresh = lax.ppermute(both, MP, moves)
+    fresh_far = swapped(fresh, "mp_2", 1)
+
     kept_heads, given_heads = attend(
         where,
         queries,
         (near_keys, far_keys, near_values, far_values),
         choice,
         own_mask,
-        fresh,
-    )
-
-    last_row = (row % STEP == span_row - 1).astype(jnp.float32)[None, :]
+        (fresh, fresh_far),
+    )
+
     parts = finish(
         where,
         kept_heads,
@@ -614,14 +663,14 @@
         pay,
         last_row,
     )
-    parts = [parts[0]] + [turned(parts[k], True, k) for k in (1, 2, 3)]
-    sums = add_first(parts)
+    moved = [parts[0]]
+    for k in (1, 2, 3):
+        moved.append(turned(parts[k], True, k))
+    sums = add_first(moved)
     sums = [sums[0]] + [turned(sums[k], False, k) for k in (1, 2, 3)]
-    live_rows = (row % STEP < span_row).astype(jnp.float32)
-    live_rows = jnp.broadcast_to(live_rows[:, None], (ROWS, HD))
     kept_sums, given_sums = add_second(where, live_rows, sums)
     scored_rows, rewards = settle(where, kept_sums, swapped(given_sums, "mp_2", 1))
-    rewards = jnp.sum(rewards.reshape(cand_here, STEP), axis=1)
+    rewards = rewards[0, :cand_here]
 
     expanded = place(growth_place_mapping, survivors)
     return (scored_rows, rewards, expanded)

time: 169 us -> 167 us (0.988)
  waiting for transfers between devices: 50 us -> 53.5 us
  local copies, waits for them, and re-layouts: 5 us -> 3.01 us
  starting transfers between devices: 59.3 us -> 57.4 us
    pallas_call x1, Pallas kernels: 11.3 us -> 8.85 us  [attend(): pl.pallas_call(attend_kernel, out_shape=(shaped(HALF, FEAT), shaped(HALF,...]
    ppermute x2 -> x1, waiting for transfers between devices: 2.02 us -> 3.86 us  [local(): fresh = lax.ppermute(both, MP, moves)]
    pallas_call x8 -> x9, Pallas kernels: 10.7 us -> 12.5 us  [call(): pl.pallas_call(kernel, out_shape=tuple(outs), in_specs=specs, out_specs=(...]
    ppermute x12 -> x13, waiting for transfers between devices: 3.19 us -> 4.26 us  [swapped(): return lax.ppermute(x, axis, [(i, i ^ bit) for i in range(size)])]
    ppermute x2 -> x1, starting transfers between devices: 4.29 us -> 3.27 us  [local(): fresh = lax.ppermute(both, MP, moves)]
    ppermute x12 -> x13, starting transfers between devices: 10.3 us -> 9.5 us  [swapped(): return lax.ppermute(x, axis, [(i, i ^ bit) for i in range(size)])]
  transfers between devices with their start and end apart: 33 -> 33, of which waited for: 15 -> 16; matrix products, arithmetic and copies ran while one was open for 3% -> 1% of each run, Pallas kernels for 17% -> 17%
where the time goes in v1:
time: 167 us; the launch traced here: 165 us
  starting transfers between devices  57.4 us (34%)
  waiting for transfers between devices  53.5 us (32%)
  Pallas kernels  36 us (22%)
  between operations  14.3 us (9%)
  local copies, waits for them, and re-layouts  3.01 us (2%)
    ppermute x12, waiting for transfers between devices, turned(): return lax.ppermute(x, MP, moves)  42.1 us
    ppermute x12, starting transfers between devices, turned(): return lax.ppermute(x, MP, moves)  19.9 us
    ppermute x4, starting transfers between devices, over_groups(): return lax.ppermute(x, ('group', 'mp_2'), moves)  13.6 us
    pallas_call x9, Pallas kernels, call(): pl.pallas_call(kernel, out_shape=tuple(outs), in_specs=specs, out_specs=(...  12.5 us
    all_to_all x2, starting transfers between devices, exchange(): return lax.all_to_all(x, axis, split_axis=0, concat_axis=0, tiled=True)  11.1 us
    ppermute x13, starting transfers between devices, swapped(): return lax.ppermute(x, axis, [(i, i ^ bit) for i in range(size)])  9.5 us
    pallas_call x1, Pallas kernels, project(): pl.pallas_call(project_kernel, out_shape=(jax.ShapeDtypeStruct((ROWS, FEA...  9.39 us
    pallas_call x1, Pallas kernels, attend(): pl.pallas_call(attend_kernel, out_shape=(shaped(HALF, FEAT), shaped(HALF,...  8.85 us
  transfers between devices with their start and end apart: 33, of which 16 were waited for; matrix products, arithmetic and copies ran while one was open for 1% of the time, Pallas kernels for 17%

profile of v1, /device:TPU:1, one launch (start us, length us, event | category | flops | bytes accessed | tf_op | source)
XLA Modules:
  0.0 165.2 jit_solution(17471967180557148988)
XLA Ops:
  7.2 3.0 %shard_map.143 = (bf16[16,2,128,128]{3,2,1,0:T(8,128)(2,1)}, bf16[16,2,128,128]{3,2,1,0:T(8,128)(2,1)}, bf16[2,2,128,1024]{3,2,1,0:T(8,128)(2,1)}) custom-call(s32[2]{0:T(128)} %kept_ref.1, bf16[2,2,128,1024]{3,2,1,0:T(8,128)(2,1)} %memo_ref.1), custom_call_target="tpu_custom_call" | custom-call | flops 4194304 | bytes 6291456 | tf_op jit(solution)/shard_map/pallas_call | solution.py:44
  10.3 3.3 %collective-permute-start.22 = (bf16[256,8192]{1,0:T(8,128)(2,1)}, bf16[256,8192]{1,0:T(8,128)(2,1)}, u32[]{:S(2)}, u32[]{:S(2)}) collective-permute-start(bf16[256,8192]{1,0:T(8,128)(2,1)} %wo_ref.1), channel_id=1, source_target_pairs={{0,1},{1,0},{2,3},{3,2},{4,5},{5,4},{6,7},{7,6},{8,9},{9,8},{10,11... | collective-permute-start | bytes 12582920 | tf_op jit(solution)/shard_map/ppermute | solution.py:574
  13.6 5.0 %all-to-all-start = ((bf16[16,2,128,128]{3,2,1,0:T(8,128)(2,1)}), bf16[16,2,128,128]{3,2,1,0:T(8,128)(2,1)S(1)}, u32[]{:S(2)}, u32[]{:S(2)}) async-start(bf16[16,2,128,128]{3,2,1,0:T(8,128)(2,1)} %get-tuple-element.41), calls=%async_computation | async-start | bytes 2097152 | tf_op jit(solution)/shard_map/all_to_all | solution.py:569
  20.7 5.6 %collective-permute-start.2 = (bf16[2,32,256]{2,1,0:T(8,128)(2,1)S(1)}, bf16[2,32,256]{2,1,0:T(8,128)(2,1)S(1)}, u32[]{:S(2)}, u32[]{:S(2)}) collective-permute-start(bf16[2,32,256]{2,1,0:T(8,128)(2,1)S(1)} %get-tuple-element.36), channel_id=1, source_target_pairs={{0,32},{1,225},{32,64},{33,1},{64,96},{65,33},{96,128},{97,65},{12... | collective-permute-start | bytes 98312 | tf_op jit(solution)/shard_map/ppermute | solution.py:565
  28.0 6.4 %collective-permute-start.5 = (bf16[2,32,256]{2,1,0:T(8,128)(2,1)S(1)}, bf16[2,32,256]{2,1,0:T(8,128)(2,1)S(1)}, u32[]{:S(2)}, u32[]{:S(2)}) collective-permute-start(bf16[2,32,256]{2,1,0:T(8,128)(2,1)S(1)} %get-tuple-element.39), channel_id=1, source_target_pairs={{0,0},{1,129},{32,32},{33,161},{64,64},{65,193},{96,96},{97,225},{... | collective-permute-start | bytes 98312 | tf_op jit(solution)/shard_map/ppermute | solution.py:565
  34.4 3.3 %collective-permute-done.5.refs_3_ = bf16[2,32,256]{2,1,0:T(8,128)(2,1)S(1)} collective-permute-done((bf16[2,32,256]{2,1,0:T(8,128)(2,1)S(1)}, bf16[2,32,256]{2,1,0:T(8,128)(2,1)S(1)}, u32[]{:S(2)}, u32[]{:S(2)}) %collective-permute-start.5) | collective-permute-done | bytes 32800 | tf_op jit(solution)/shard_map/ppermute | solution.py:565
  43.5 2.4 %collective-permute-done.7 = bf16[2,144,256]{2,1,0:T(8,128)(2,1)S(1)} collective-permute-done((bf16[2,144,256]{2,1,0:T(8,128)(2,1)S(1)}, bf16[2,144,256]{2,1,0:T(8,128)(2,1)S(1)}, u32[]{:S(2)}, u32[]{:S(2)}) %collective-permute-start.7) | collective-permute-done | bytes 147488 | tf_op jit(solution)/shard_map/ppermute | solution.py:556
  47.5 6.0 %all-to-all-start.1 = ((bf16[16,2,128,128]{3,2,1,0:T(8,128)(2,1)}), bf16[16,2,128,128]{3,2,1,0:T(8,128)(2,1)S(1)}, u32[]{:S(2)}, u32[]{:S(2)}) async-start(bf16[16,2,128,128]{3,2,1,0:T(8,128)(2,1)} %get-tuple-element.42), calls=%async_computation.1 | async-start | bytes 2097152 | tf_op jit(solution)/shard_map/all_to_all | solution.py:569
  53.5 2.9 %collective-permute-start.10 = (bf16[4,2,144,256]{3,2,1,0:T(8,128)(2,1)S(1)}, bf16[4,2,144,256]{3,2,1,0:T(8,128)(2,1)}, u32[]{:S(2)}, u32[]{:S(2)}) collective-permute-start(bf16[4,2,144,256]{3,2,1,0:T(8,128)(2,1)S(1)} %pad_maximum_fusion.refs_0_), channel_id=1, source_target_pairs={{0,16},{1,5},{2,18},{3,7},{4,20},{5,1},{6,22},{7,3},{8,24},{9,13},... | collective-permute-start | bytes 1769480 | tf_op jit(solution)/shard_map/ppermute | solution.py:556
  57.8 17.9 %collective-permute-done.10.refs_2_ = bf16[4,2,144,256]{3,2,1,0:T(8,128)(2,1)} collective-permute-done((bf16[4,2,144,256]{3,2,1,0:T(8,128)(2,1)S(1)}, bf16[4,2,144,256]{3,2,1,0:T(8,128)(2,1)}, u32[]{:S(2)}, u32[]{:S(2)}) %collective-permute-start.10) | collective-permute-done | bytes 589856 | tf_op jit(solution)/shard_map/ppermute | solution.py:556
  75.7 3.8 %collective-permute-done.11.refs_3_ = bf16[4,2,144,256]{3,2,1,0:T(8,128)(2,1)} collective-permute-done((bf16[4,2,144,256]{3,2,1,0:T(8,128)(2,1)S(1)}, bf16[4,2,144,256]{3,2,1,0:T(8,128)(2,1)}, u32[]{:S(2)}, u32[]{:S(2)}) %collective-permute-start.11) | collective-permute-done | bytes 589856 | tf_op jit(solution)/shard_map/ppermute | solution.py:556
  81.8 9.4 %project.1 = (bf16[256,256]{1,0:T(8,128)(2,1)}, bf16[64,256]{1,0:T(8,128)(2,1)}, f32[1,8192]{1,0:T(1,128)}) custom-call(s32[4]{0:T(128)} %copy-done.3, bf16[4,2,144,256]{3,2,1,0:T(8,128)(2,1)} %copy-done.10, bf16[4,2,144,256]{3,2,1,0:T(8,128)(2,1)} %collective-permute-done.9.refs_1_, bf16[4,2,144,256]{3,2,1,0:T(8,128)(2,1)} %collective-permute-done.10.refs_2_, ...), custom_call_target="tpu_custom_call" | custom-call | flops 1342177280 | bytes 10485760 | tf_op jit(solution)/shard_map/project/pallas_call | solution.py:260
  93.5 3.3 %collective-permute-start.19 = (bf16[128,256]{1,0:T(8,128)(2,1)S(1)}, bf16[128,256]{1,0:T(8,128)(2,1)S(1)}, u32[]{:S(2)}, u32[]{:S(2)}) collective-permute-start(bf16[128,256]{1,0:T(8,128)(2,1)S(1)} %pad_maximum_fusion.1), channel_id=1, source_target_pairs={{0,0},{1,2},{16,1},{17,3},{2,4},{3,6},{18,5},{19,7},{4,8},{5,10},{... | collective-permute-start | bytes 196616 | tf_op jit(solution)/shard_map/ppermute | solution.py:645
  96.8 3.9 %collective-permute-done.19.fresh_ref = bf16[128,256]{1,0:T(8,128)(2,1)S(1)} collective-permute-done((bf16[128,256]{1,0:T(8,128)(2,1)S(1)}, bf16[128,256]{1,0:T(8,128)(2,1)S(1)}, u32[]{:S(2)}, u32[]{:S(2)}) %collective-permute-start.19) | collective-permute-done | bytes 65568 | tf_op jit(solution)/shard_map/ppermute | solution.py:645
  104.1 8.9 %attend.1 = (bf16[128,256]{1,0:T(8,128)(2,1)S(1)}, bf16[128,256]{1,0:T(8,128)(2,1)S(1)}) custom-call(s32[4]{0:T(128)S(1)} %copy-done.4, bf16[256,256]{1,0:T(8,128)(2,1)S(1)} %copy-done.6, bf16[16,2,128,128]{3,2,1,0:T(8,128)(2,1)S(1)} %all-to-all-done.near_keys, bf16[16,2,128,128]{3,2,1,0:T(8,128)(2,1)S(1)} %collective-permute-done.16.far_keys, ...), custom_call_target="tpu_custom_call" | custom-call | flops 4294967296 | bytes 5242880 | tf_op jit(solution)/shard_map/attend/pallas_call | solution.py:395
  114.5 4.9 %shard_map.144 = (bf16[4,272,256]{2,1,0:T(8,128)(2,1)S(1)}, bf16[4,272,256]{2,1,0:T(8,128)(2,1)S(1)}, bf16[4,272,256]{2,1,0:T(8,128)(2,1)S(1)}, bf16[4,272,256]{2,1,0:T(8,128)(2,1)S(1)}) custom-call(s32[4]{0:T(128)S(1)} %copy-done.5, bf16[128,256]{1,0:T(8,128)(2,1)S(1)} %get-tuple-element.46.near_ref, bf16[128,256]{1,0:T(8,128)(2,1)S(1)} %collective-permute-done.21.far_ref, ...), custom_call_target="tpu_custom_call" | custom-call | flops 1073741824 | bytes 4456448 | tf_op jit(solution)/shard_map/pallas_call | solution.py:44
  119.3 2.9 %collective-permute-start.23 = (bf16[4,272,256]{2,1,0:T(8,128)(2,1)S(1)}, bf16[4,272,256]{2,1,0:T(8,128)(2,1)S(1)}, u32[]{:S(2)}, u32[]{:S(2)}) collective-permute-start(bf16[4,272,256]{2,1,0:T(8,128)(2,1)S(1)} %get-tuple-element.51), channel_id=1, source_target_pairs={{0,2},{1,9},{2,4},{3,11},{4,6},{5,13},{6,0},{7,15},{8,10},{9,17},{... | collective-permute-start | bytes 1671176 | tf_op jit(solution)/shard_map/ppermute | solution.py:556
  122.2 3.8 %collective-permute-start.24 = (bf16[4,272,256]{2,1,0:T(8,128)(2,1)S(1)}, bf16[4,272,256]{2,1,0:T(8,128)(2,1)S(1)}, u32[]{:S(2)}, u32[]{:S(2)}) collective-permute-start(bf16[4,272,256]{2,1,0:T(8,128)(2,1)S(1)} %get-tuple-element.52), channel_id=1, source_target_pairs={{0,4},{1,17},{2,6},{3,19},{4,0},{5,21},{6,2},{7,23},{8,12},{9,25},... | collective-permute-start | bytes 1671176 | tf_op jit(solution)/shard_map/ppermute | solution.py:556
  126.0 5.7 %collective-permute-done.23.refs_1_ = bf16[4,272,256]{2,1,0:T(8,128)(2,1)S(1)} collective-permute-done((bf16[4,272,256]{2,1,0:T(8,128)(2,1)S(1)}, bf16[4,272,256]{2,1,0:T(8,128)(2,1)S(1)}, u32[]{:S(2)}, u32[]{:S(2)}) %collective-permute-start.23) | collective-permute-done | bytes 557088 | tf_op jit(solution)/shard_map/ppermute | solution.py:556
  131.7 7.2 %collective-permute-done.24.refs_2_ = bf16[4,272,256]{2,1,0:T(8,128)(2,1)S(1)} collective-permute-done((bf16[4,272,256]{2,1,0:T(8,128)(2,1)S(1)}, bf16[4,272,256]{2,1,0:T(8,128)(2,1)S(1)}, u32[]{:S(2)}, u32[]{:S(2)}) %collective-permute-start.24) | collective-permute-done | bytes 557088 | tf_op jit(solution)/shard_map/ppermute | solution.py:556
  139.3 2.5 %collective-permute-start.27 = (bf16[272,256]{1,0:T(8,128)(2,1)S(1)}, bf16[272,256]{1,0:T(8,128)(2,1)S(1)}, u32[]{:S(2)}, u32[]{:S(2)}) collective-permute-start(bf16[272,256]{1,0:T(8,128)(2,1)S(1)} %get-tuple-element.56), channel_id=1, source_target_pairs={{0,16},{1,5},{2,18},{3,7},{4,20},{5,1},{6,22},{7,3},{8,24},{9,13},... | collective-permute-start | bytes 417800 | tf_op jit(solution)/shard_map/ppermute | solution.py:556
  142.2 3.7 %collective-permute-done.26.refs_1_ = bf16[272,256]{1,0:T(8,128)(2,1)S(1)} collective-permute-done((bf16[272,256]{1,0:T(8,128)(2,1)S(1)}, bf16[272,256]{1,0:T(8,128)(2,1)S(1)}, u32[]{:S(2)}, u32[]{:S(2)}) %collective-permute-start.26) | collective-permute-done | bytes 139296 | tf_op jit(solution)/shard_map/ppermute | solution.py:556
  147.1 3.3 %collective-permute-start.29 = (bf16[144,256]{1,0:T(8,128)(2,1)S(1)}, bf16[144,256]{1,0:T(8,128)(2,1)S(1)}, u32[]{:S(2)}, u32[]{:S(2)}) collective-permute-start(bf16[144,256]{1,0:T(8,128)(2,1)S(1)} %get-tuple-element.59), channel_id=1, source_target_pairs={{0,1},{1,0},{2,3},{3,2},{4,5},{5,4},{6,7},{7,6},{8,9},{9,8},{10,11... | collective-permute-start | bytes 221192 | tf_op jit(solution)/shard_map/ppermute | solution.py:574
  153.1 5.2 %place.1 = bf16[2,3,128,1024]{3,2,1,0:T(8,128)(2,1)} custom-call(s32[3]{0:T(128)} %label_ref.1, bf16[16,2,128,1024]{3,2,1,0:T(8,128)(2,1)} %all-gather.2.cloned.1.call-done.in_ref), custom_call_target="tpu_custom_call" | custom-call | flops 4194304 | bytes 3145728 | tf_op jit(solution)/shard_map/place/pallas_call | solution.py:177
  (92 shorter events, 26.9 us)
Async XLA Ops:
  7.2 145.9 %all-gather.2.cloned.1.call-start = ((), (), s32[]{:S(2)}) async-start(), calls=%async_computation.2 | async-start | bytes 9437184 | tf_op jit(solution)/shard_map/all_gather | solution.py:595
  10.3 104.1 %collective-permute-start.22 = (bf16[256,8192]{1,0:T(8,128)(2,1)}, bf16[256,8192]{1,0:T(8,128)(2,1)}, u32[]{:S(2)}, u32[]{:S(2)}) collective-permute-start(bf16[256,8192]{1,0:T(8,128)(2,1)} %wo_ref.1), channel_id=1, source_target_pairs={{0,1},{1,0},{2,3},{3,2},{4,5},{5,4},{6,7},{7,6},{8,9},{9,8},{10,11... | collective-permute-start | bytes 12582920 | tf_op jit(solution)/shard_map/ppermute | solution.py:574
  13.6 33.9 %all-to-all-start = ((bf16[16,2,128,128]{3,2,1,0:T(8,128)(2,1)}), bf16[16,2,128,128]{3,2,1,0:T(8,128)(2,1)S(1)}, u32[]{:S(2)}, u32[]{:S(2)}) async-start(bf16[16,2,128,128]{3,2,1,0:T(8,128)(2,1)} %get-tuple-element.41), calls=%async_computation | async-start | bytes 2097152 | tf_op jit(solution)/shard_map/all_to_all | solution.py:569
  19.9 8.1 %collective-permute-start = (bf16[16,256]{1,0:T(8,128)(2,1)S(1)}, bf16[16,256]{1,0:T(8,128)(2,1)S(1)}, u32[]{:S(2)}, u32[]{:S(2)}) collective-permute-start(bf16[16,256]{1,0:T(8,128)(2,1)S(1)} %maximum_maximum_fusion.extra_ref), channel_id=1, source_target_pairs={{0,1},{1,0},{2,3},{3,2},{4,5},{5,4},{6,7},{7,6},{8,9},{9,8},{10,11... | collective-permute-start | bytes 24584 | tf_op jit(solution)/shard_map/ppermute | solution.py:574
  20.7 13.6 %collective-permute-start.2 = (bf16[2,32,256]{2,1,0:T(8,128)(2,1)S(1)}, bf16[2,32,256]{2,1,0:T(8,128)(2,1)S(1)}, u32[]{:S(2)}, u32[]{:S(2)}) collective-permute-start(bf16[2,32,256]{2,1,0:T(8,128)(2,1)S(1)} %get-tuple-element.36), channel_id=1, source_target_pairs={{0,32},{1,225},{32,64},{33,1},{64,96},{65,33},{96,128},{97,65},{12... | collective-permute-start | bytes 98312 | tf_op jit(solution)/shard_map/ppermute | solution.py:565
  26.3 8.0 %collective-permute-start.3 = (bf16[2,32,256]{2,1,0:T(8,128)(2,1)S(1)}, bf16[2,32,256]{2,1,0:T(8,128)(2,1)S(1)}, u32[]{:S(2)}, u32[]{:S(2)}) collective-permute-start(bf16[2,32,256]{2,1,0:T(8,128)(2,1)S(1)} %get-tuple-element.37), channel_id=1, source_target_pairs={{0,64},{1,193},{32,96},{33,225},{64,128},{65,1},{96,160},{97,33},{... | collective-permute-start | bytes 98312 | tf_op jit(solution)/shard_map/ppermute | solution.py:565
  27.5 6.9 %collective-permute-start.4 = (bf16[2,32,256]{2,1,0:T(8,128)(2,1)S(1)}, bf16[2,32,256]{2,1,0:T(8,128)(2,1)S(1)}, u32[]{:S(2)}, u32[]{:S(2)}) collective-permute-start(bf16[2,32,256]{2,1,0:T(8,128)(2,1)S(1)} %get-tuple-element.38), channel_id=1, source_target_pairs={{0,96},{1,161},{32,128},{33,193},{64,160},{65,225},{96,192},{97,1}... | collective-permute-start | bytes 98312 | tf_op jit(solution)/shard_map/ppermute | solution.py:565
  28.0 9.7 %collective-permute-start.5 = (bf16[2,32,256]{2,1,0:T(8,128)(2,1)S(1)}, bf16[2,32,256]{2,1,0:T(8,128)(2,1)S(1)}, u32[]{:S(2)}, u32[]{:S(2)}) collective-permute-start(bf16[2,32,256]{2,1,0:T(8,128)(2,1)S(1)} %get-tuple-element.39), channel_id=1, source_target_pairs={{0,0},{1,129},{32,32},{33,161},{64,64},{65,193},{96,96},{97,225},{... | collective-permute-start | bytes 98312 | tf_op jit(solution)/shard_map/ppermute | solution.py:565
  37.7 5.8 %collective-permute-start.6 = (bf16[2,144,256]{2,1,0:T(8,128)(2,1)S(1)}, bf16[2,144,256]{2,1,0:T(8,128)(2,1)S(1)}, u32[]{:S(2)}, u32[]{:S(2)}) collective-permute-start(bf16[2,144,256]{2,1,0:T(8,128)(2,1)S(1)} %shard_map.142), channel_id=1, source_target_pairs={{0,2},{1,9},{2,4},{3,11},{4,6},{5,13},{6,0},{7,15},{8,10},{9,17},{... | collective-permute-start | bytes 442376 | tf_op jit(solution)/shard_map/ppermute | solution.py:556
  39.4 6.6 %collective-permute-start.7 = (bf16[2,144,256]{2,1,0:T(8,128)(2,1)S(1)}, bf16[2,144,256]{2,1,0:T(8,128)(2,1)S(1)}, u32[]{:S(2)}, u32[]{:S(2)}) collective-permute-start(bf16[2,144,256]{2,1,0:T(8,128)(2,1)S(1)} %shard_map.142), channel_id=1, source_target_pairs={{0,4},{1,17},{2,6},{3,19},{4,0},{5,21},{6,2},{7,23},{8,12},{9,25},... | collective-permute-start | bytes 442376 | tf_op jit(solution)/shard_map/ppermute | solution.py:556
  46.2 11.1 %collective-permute-start.9 = (bf16[4,2,144,256]{3,2,1,0:T(8,128)(2,1)S(1)}, bf16[4,2,144,256]{3,2,1,0:T(8,128)(2,1)}, u32[]{:S(2)}, u32[]{:S(2)}) collective-permute-start(bf16[4,2,144,256]{3,2,1,0:T(8,128)(2,1)S(1)} %pad_maximum_fusion.refs_0_), channel_id=1, source_target_pairs={{0,8},{1,3},{2,10},{3,5},{4,12},{5,7},{6,14},{7,1},{8,16},{9,11},{... | collective-permute-start | bytes 1769480 | tf_op jit(solution)/shard_map/ppermute | solution.py:556
  47.5 33.3 %all-to-all-start.1 = ((bf16[16,2,128,128]{3,2,1,0:T(8,128)(2,1)}), bf16[16,2,128,128]{3,2,1,0:T(8,128)(2,1)S(1)}, u32[]{:S(2)}, u32[]{:S(2)}) async-start(bf16[16,2,128,128]{3,2,1,0:T(8,128)(2,1)} %get-tuple-element.42), calls=%async_computation.1 | async-start | bytes 2097152 | tf_op jit(solution)/shard_map/all_to_all | solution.py:569
  53.5 22.2 %collective-permute-start.10 = (bf16[4,2,144,256]{3,2,1,0:T(8,128)(2,1)S(1)}, bf16[4,2,144,256]{3,2,1,0:T(8,128)(2,1)}, u32[]{:S(2)}, u32[]{:S(2)}) collective-permute-start(bf16[4,2,144,256]{3,2,1,0:T(8,128)(2,1)S(1)} %pad_maximum_fusion.refs_0_), channel_id=1, source_target_pairs={{0,16},{1,5},{2,18},{3,7},{4,20},{5,1},{6,22},{7,3},{8,24},{9,13},... | collective-permute-start | bytes 1769480 | tf_op jit(solution)/shard_map/ppermute | solution.py:556
  56.4 23.1 %collective-permute-start.11 = (bf16[4,2,144,256]{3,2,1,0:T(8,128)(2,1)S(1)}, bf16[4,2,144,256]{3,2,1,0:T(8,128)(2,1)}, u32[]{:S(2)}, u32[]{:S(2)}) collective-permute-start(bf16[4,2,144,256]{3,2,1,0:T(8,128)(2,1)S(1)} %pad_maximum_fusion.refs_0_), channel_id=1, source_target_pairs={{0,24},{1,7},{2,26},{3,1},{4,28},{5,3},{6,30},{7,5},{8,0},{9,15},{... | collective-permute-start | bytes 1769480 | tf_op jit(solution)/shard_map/ppermute | solution.py:556
  57.3 22.5 %collective-permute-start.12 = (bf16[4,2,144,256]{3,2,1,0:T(8,128)(2,1)S(1)}, bf16[4,2,144,256]{3,2,1,0:T(8,128)(2,1)S(1)}, u32[]{:S(2)}, u32[]{:S(2)}) collective-permute-start(bf16[4,2,144,256]{3,2,1,0:T(8,128)(2,1)S(1)} %pad_maximum_fusion.refs_0_), channel_id=1, source_target_pairs={{0,1},{1,0},{2,3},{3,2},{4,5},{5,4},{6,7},{7,6},{8,9},{9,8},{10,11... | collective-permute-start | bytes 1769480 | tf_op jit(solution)/shard_map/ppermute | solution.py:574
  57.3 23.5 %collective-permute-start.13 = (bf16[4,2,144,256]{3,2,1,0:T(8,128)(2,1)}, bf16[4,2,144,256]{3,2,1,0:T(8,128)(2,1)}, u32[]{:S(2)}, u32[]{:S(2)}) collective-permute-start(bf16[4,2,144,256]{3,2,1,0:T(8,128)(2,1)} %collective-permute-done.9.refs_1_), channel_id=1, source_target_pairs={{0,1},{1,0},{2,3},{3,2},{4,5},{5,4},{6,7},{7,6},{8,9},{9,8},{10,11... | collective-permute-start | bytes 1769480 | tf_op jit(solution)/shard_map/ppermute | solution.py:574
  80.6 22.0 %collective-permute-start.16 = (bf16[16,2,128,128]{3,2,1,0:T(8,128)(2,1)S(1)}, bf16[16,2,128,128]{3,2,1,0:T(8,128)(2,1)S(1)}, u32[]{:S(2)}, u32[]{:S(2)}) collective-permute-start(bf16[16,2,128,128]{3,2,1,0:T(8,128)(2,1)S(1)} %all-to-all-done.near_keys), channel_id=1, source_target_pairs={{0,1},{1,0},{2,3},{3,2},{4,5},{5,4},{6,7},{7,6},{8,9},{9,8},{10,11... | collective-permute-start | bytes 3145736 | tf_op jit(solution)/shard_map/ppermute | solution.py:574
  80.8 21.8 %collective-permute-start.17 = (bf16[16,2,128,128]{3,2,1,0:T(8,128)(2,1)S(1)}, bf16[16,2,128,128]{3,2,1,0:T(8,128)(2,1)}, u32[]{:S(2)}, u32[]{:S(2)}) collective-permute-start(bf16[16,2,128,128]{3,2,1,0:T(8,128)(2,1)S(1)} %all-to-all-done.1.near_values), channel_id=1, source_target_pairs={{0,1},{1,0},{2,3},{3,2},{4,5},{5,4},{6,7},{7,6},{8,9},{9,8},{10,11... | collective-permute-start | bytes 3145736 | tf_op jit(solution)/shard_map/ppermute | solution.py:574
  93.5 7.1 %collective-permute-start.19 = (bf16[128,256]{1,0:T(8,128)(2,1)S(1)}, bf16[128,256]{1,0:T(8,128)(2,1)S(1)}, u32[]{:S(2)}, u32[]{:S(2)}) collective-permute-start(bf16[128,256]{1,0:T(8,128)(2,1)S(1)} %pad_maximum_fusion.1), channel_id=1, source_target_pairs={{0,0},{1,2},{16,1},{17,3},{2,4},{3,6},{18,5},{19,7},{4,8},{5,10},{... | collective-permute-start | bytes 196616 | tf_op jit(solution)/shard_map/ppermute | solution.py:645
  119.3 12.4 %collective-permute-start.23 = (bf16[4,272,256]{2,1,0:T(8,128)(2,1)S(1)}, bf16[4,272,256]{2,1,0:T(8,128)(2,1)S(1)}, u32[]{:S(2)}, u32[]{:S(2)}) collective-permute-start(bf16[4,272,256]{2,1,0:T(8,128)(2,1)S(1)} %get-tuple-element.51), channel_id=1, source_target_pairs={{0,2},{1,9},{2,4},{3,11},{4,6},{5,13},{6,0},{7,15},{8,10},{9,17},{... | collective-permute-start | bytes 1671176 | tf_op jit(solution)/shard_map/ppermute | solution.py:556
  122.2 16.7 %collective-permute-start.24 = (bf16[4,272,256]{2,1,0:T(8,128)(2,1)S(1)}, bf16[4,272,256]{2,1,0:T(8,128)(2,1)S(1)}, u32[]{:S(2)}, u32[]{:S(2)}) collective-permute-start(bf16[4,272,256]{2,1,0:T(8,128)(2,1)S(1)} %get-tuple-element.52), channel_id=1, source_target_pairs={{0,4},{1,17},{2,6},{3,19},{4,0},{5,21},{6,2},{7,23},{8,12},{9,25},... | collective-permute-start | bytes 1671176 | tf_op jit(solution)/shard_map/ppermute | solution.py:556
  126.0 12.9 %collective-permute-start.25 = (bf16[4,272,256]{2,1,0:T(8,128)(2,1)S(1)}, bf16[4,272,256]{2,1,0:T(8,128)(2,1)S(1)}, u32[]{:S(2)}, u32[]{:S(2)}) collective-permute-start(bf16[4,272,256]{2,1,0:T(8,128)(2,1)S(1)} %get-tuple-element.53), channel_id=1, source_target_pairs={{0,6},{1,25},{2,0},{3,27},{4,2},{5,29},{6,4},{7,31},{8,14},{9,1},{... | collective-permute-start | bytes 1671176 | tf_op jit(solution)/shard_map/ppermute | solution.py:556
  139.2 6.7 %collective-permute-start.26 = (bf16[272,256]{1,0:T(8,128)(2,1)S(1)}, bf16[272,256]{1,0:T(8,128)(2,1)S(1)}, u32[]{:S(2)}, u32[]{:S(2)}) collective-permute-start(bf16[272,256]{1,0:T(8,128)(2,1)S(1)} %get-tuple-element.55), channel_id=1, source_target_pairs={{0,8},{1,3},{2,10},{3,5},{4,12},{5,7},{6,14},{7,1},{8,16},{9,11},{... | collective-permute-start | bytes 417800 | tf_op jit(solution)/shard_map/ppermute | solution.py:556
  139.3 6.6 %collective-permute-start.27 = (bf16[272,256]{1,0:T(8,128)(2,1)S(1)}, bf16[272,256]{1,0:T(8,128)(2,1)S(1)}, u32[]{:S(2)}, u32[]{:S(2)}) collective-permute-start(bf16[272,256]{1,0:T(8,128)(2,1)S(1)} %get-tuple-element.56), channel_id=1, source_target_pairs={{0,16},{1,5},{2,18},{3,7},{4,20},{5,1},{6,22},{7,3},{8,24},{9,13},... | collective-permute-start | bytes 417800 | tf_op jit(solution)/shard_map/ppermute | solution.py:556
  (23 other events, 250.7 us)
Sparse Core Ops, SparseCore 0:
  10.4 99.7 all-gather.1

commit v2 on v1

--- a/solution.py
+++ b/solution.py
@@ -249,6 +249,7 @@
         D // step,
         multiply,
         (jnp.zeros((ROWS, FEAT), jnp.float32), jnp.zeros((ROWS, 64), jnp.float32)),
+        unroll=4,
     )
     total = squares[...]
     down = lax.rsqrt(jnp.sum(total, axis=1, keepdims=True) / D + epsilon)
@@ -356,7 +357,7 @@
     copies[6].wait()
     copies[0].wait()
     copies[1].wait()
-    lax.fori_loop(0, CHIPS, score, 0, unroll=2)
+    lax.fori_loop(0, CHIPS, score, 0, unroll=16)
     top = jnp.max(tops[...], axis=1, keepdims=True)
     tops[...] = jnp.broadcast_to(top, (rows, HD))
     own_mass = jnp.where(own_mask, jnp.exp2(own_score - top), 0.0)
@@ -382,7 +383,7 @@
 
     copies[2].wait()
     copies[3].wait()
-    lax.fori_loop(0, CHIPS, weigh, 0, unroll=2)
+    lax.fori_loop(0, CHIPS, weigh, 0, unroll=16)
     attended = sums[...] / jnp.sum(masses[...], axis=1, keepdims=True)
     sums[...] = attended
     for mine, out_ref in ((core, keep_ref), (1 - core, give_ref)):
@@ -457,7 +458,7 @@
             reward[...] += paid[:, :HD] + paid[:, HD:]
             return 0
 
-        lax.fori_loop(0, SIDE, multiply, 0, unroll=2)
+        lax.fori_loop(0, SIDE, multiply, 0, unroll=4)
     last = jnp.where(core == 0, last_ref[:, :HALF], last_ref[:, HALF:])
     row = jnp.sum(reward[...].T, axis=0, keepdims=True) * last
     terms = in_terms(jnp.concatenate([row, jnp.zeros_like(row)], axis=1))

time: 167 us -> 166 us (level)
  transfers between devices with their start and end apart: 33 -> 33, of which waited for: 16 -> 16; matrix products, arithmetic and copies ran while one was open for 1% -> 1% of each run, Pallas kernels for 17% -> 16%
where the time goes in v2:
time: 166 us; the launch traced here: 164 us
  starting transfers between devices  57.5 us (35%)
  waiting for transfers between devices  53.4 us (32%)
  Pallas kernels  35.3 us (21%)
  between operations  14.3 us (9%)
  local copies, waits for them, and re-layouts  3.01 us (2%)
    ppermute x12, waiting for transfers between devices, turned(): return lax.ppermute(x, MP, moves)  41.9 us
    ppermute x12, starting transfers between devices, turned(): return lax.ppermute(x, MP, moves)  19.9 us
    ppermute x4, starting transfers between devices, over_groups(): return lax.ppermute(x, ('group', 'mp_2'), moves)  13.6 us
    pallas_call x9, Pallas kernels, call(): pl.pallas_call(kernel, out_shape=tuple(outs), in_specs=specs, out_specs=(...  11.3 us
    all_to_all x2, starting transfers between devices, exchange(): return lax.all_to_all(x, axis, split_axis=0, concat_axis=0, tiled=True)  11.1 us
    pallas_call x1, Pallas kernels, attend(): pl.pallas_call(attend_kernel, out_shape=(shaped(HALF, FEAT), shaped(HALF,...  10.5 us
    ppermute x13, starting transfers between devices, swapped(): return lax.ppermute(x, axis, [(i, i ^ bit) for i in range(size)])  9.58 us
    pallas_call x1, Pallas kernels, project(): pl.pallas_call(project_kernel, out_shape=(jax.ShapeDtypeStruct((ROWS, FEA...  8.25 us
  transfers between devices with their start and end apart: 33, of which 16 were waited for; matrix products, arithmetic and copies ran while one was open for 1% of the time, Pallas kernels for 16%

profile of v2, /device:TPU:1, one launch (start us, length us, event | category | flops | bytes accessed | tf_op | source)
XLA Modules:
  0.0 164.4 jit_solution(9844798341065487616)
XLA Ops:
  7.2 3.0 %shard_map.143 = (bf16[16,2,128,128]{3,2,1,0:T(8,128)(2,1)}, bf16[16,2,128,128]{3,2,1,0:T(8,128)(2,1)}, bf16[2,2,128,1024]{3,2,1,0:T(8,128)(2,1)}) custom-call(s32[2]{0:T(128)} %kept_ref.1, bf16[2,2,128,1024]{3,2,1,0:T(8,128)(2,1)} %memo_ref.1), custom_call_target="tpu_custom_call" | custom-call | flops 4194304 | bytes 6291456 | tf_op jit(solution)/shard_map/pallas_call | solution.py:44
  10.3 3.3 %collective-permute-start.22 = (bf16[256,8192]{1,0:T(8,128)(2,1)}, bf16[256,8192]{1,0:T(8,128)(2,1)}, u32[]{:S(2)}, u32[]{:S(2)}) collective-permute-start(bf16[256,8192]{1,0:T(8,128)(2,1)} %wo_ref.1), channel_id=1, source_target_pairs={{0,1},{1,0},{2,3},{3,2},{4,5},{5,4},{6,7},{7,6},{8,9},{9,8},{10,11... | collective-permute-start | bytes 12582920 | tf_op jit(solution)/shard_map/ppermute | solution.py:575
  13.6 5.0 %all-to-all-start = ((bf16[16,2,128,128]{3,2,1,0:T(8,128)(2,1)}), bf16[16,2,128,128]{3,2,1,0:T(8,128)(2,1)S(1)}, u32[]{:S(2)}, u32[]{:S(2)}) async-start(bf16[16,2,128,128]{3,2,1,0:T(8,128)(2,1)} %get-tuple-element.41), calls=%async_computation | async-start | bytes 2097152 | tf_op jit(solution)/shard_map/all_to_all | solution.py:570
  20.7 5.6 %collective-permute-start.2 = (bf16[2,32,256]{2,1,0:T(8,128)(2,1)S(1)}, bf16[2,32,256]{2,1,0:T(8,128)(2,1)S(1)}, u32[]{:S(2)}, u32[]{:S(2)}) collective-permute-start(bf16[2,32,256]{2,1,0:T(8,128)(2,1)S(1)} %get-tuple-element.36), channel_id=1, source_target_pairs={{0,32},{1,225},{32,64},{33,1},{64,96},{65,33},{96,128},{97,65},{12... | collective-permute-start | bytes 98312 | tf_op jit(solution)/shard_map/ppermute | solution.py:566
  28.0 6.4 %collective-permute-start.5 = (bf16[2,32,256]{2,1,0:T(8,128)(2,1)S(1)}, bf16[2,32,256]{2,1,0:T(8,128)(2,1)S(1)}, u32[]{:S(2)}, u32[]{:S(2)}) collective-permute-start(bf16[2,32,256]{2,1,0:T(8,128)(2,1)S(1)} %get-tuple-element.39), channel_id=1, source_target_pairs={{0,0},{1,129},{32,32},{33,161},{64,64},{65,193},{96,96},{97,225},{... | collective-permute-start | bytes 98312 | tf_op jit(solution)/shard_map/ppermute | solution.py:566
  34.4 3.3 %collective-permute-done.5.refs_3_ = bf16[2,32,256]{2,1,0:T(8,128)(2,1)S(1)} collective-permute-done((bf16[2,32,256]{2,1,0:T(8,128)(2,1)S(1)}, bf16[2,32,256]{2,1,0:T(8,128)(2,1)S(1)}, u32[]{:S(2)}, u32[]{:S(2)}) %collective-permute-start.5) | collective-permute-done | bytes 32800 | tf_op jit(solution)/shard_map/ppermute | solution.py:566
  43.5 2.4 %collective-permute-done.7 = bf16[2,144,256]{2,1,0:T(8,128)(2,1)S(1)} collective-permute-done((bf16[2,144,256]{2,1,0:T(8,128)(2,1)S(1)}, bf16[2,144,256]{2,1,0:T(8,128)(2,1)S(1)}, u32[]{:S(2)}, u32[]{:S(2)}) %collective-permute-start.7) | collective-permute-done | bytes 147488 | tf_op jit(solution)/shard_map/ppermute | solution.py:557
  47.5 6.0 %all-to-all-start.1 = ((bf16[16,2,128,128]{3,2,1,0:T(8,128)(2,1)}), bf16[16,2,128,128]{3,2,1,0:T(8,128)(2,1)S(1)}, u32[]{:S(2)}, u32[]{:S(2)}) async-start(bf16[16,2,128,128]{3,2,1,0:T(8,128)(2,1)} %get-tuple-element.42), calls=%async_computation.1 | async-start | bytes 2097152 | tf_op jit(solution)/shard_map/all_to_all | solution.py:570
  53.5 2.9 %collective-permute-start.10 = (bf16[4,2,144,256]{3,2,1,0:T(8,128)(2,1)S(1)}, bf16[4,2,144,256]{3,2,1,0:T(8,128)(2,1)}, u32[]{:S(2)}, u32[]{:S(2)}) collective-permute-start(bf16[4,2,144,256]{3,2,1,0:T(8,128)(2,1)S(1)} %pad_maximum_fusion.refs_0_), channel_id=1, source_target_pairs={{0,16},{1,5},{2,18},{3,7},{4,20},{5,1},{6,22},{7,3},{8,24},{9,13},... | collective-permute-start | bytes 1769480 | tf_op jit(solution)/shard_map/ppermute | solution.py:557
  57.8 17.9 %collective-permute-done.10.refs_2_ = bf16[4,2,144,256]{3,2,1,0:T(8,128)(2,1)} collective-permute-done((bf16[4,2,144,256]{3,2,1,0:T(8,128)(2,1)S(1)}, bf16[4,2,144,256]{3,2,1,0:T(8,128)(2,1)}, u32[]{:S(2)}, u32[]{:S(2)}) %collective-permute-start.10) | collective-permute-done | bytes 589856 | tf_op jit(solution)/shard_map/ppermute | solution.py:557
  75.7 3.8 %collective-permute-done.11.refs_3_ = bf16[4,2,144,256]{3,2,1,0:T(8,128)(2,1)} collective-permute-done((bf16[4,2,144,256]{3,2,1,0:T(8,128)(2,1)S(1)}, bf16[4,2,144,256]{3,2,1,0:T(8,128)(2,1)}, u32[]{:S(2)}, u32[]{:S(2)}) %collective-permute-start.11) | collective-permute-done | bytes 589856 | tf_op jit(solution)/shard_map/ppermute | solution.py:557
  81.8 8.3 %project.1 = (bf16[256,256]{1,0:T(8,128)(2,1)}, bf16[64,256]{1,0:T(8,128)(2,1)}, f32[1,8192]{1,0:T(1,128)}) custom-call(s32[4]{0:T(128)} %copy-done.3, bf16[4,2,144,256]{3,2,1,0:T(8,128)(2,1)} %copy-done.10, bf16[4,2,144,256]{3,2,1,0:T(8,128)(2,1)} %collective-permute-done.9.refs_1_, bf16[4,2,144,256]{3,2,1,0:T(8,128)(2,1)} %collective-permute-done.10.refs_2_, ...), custom_call_target="tpu_custom_call" | custom-call | flops 1342177280 | bytes 10485760 | tf_op jit(solution)/shard_map/project/pallas_call | solution.py:261
  92.4 3.3 %collective-permute-start.19 = (bf16[128,256]{1,0:T(8,128)(2,1)S(1)}, bf16[128,256]{1,0:T(8,128)(2,1)S(1)}, u32[]{:S(2)}, u32[]{:S(2)}) collective-permute-start(bf16[128,256]{1,0:T(8,128)(2,1)S(1)} %pad_maximum_fusion.1), channel_id=1, source_target_pairs={{0,0},{1,2},{16,1},{17,3},{2,4},{3,6},{18,5},{19,7},{4,8},{5,10},{... | collective-permute-start | bytes 196616 | tf_op jit(solution)/shard_map/ppermute | solution.py:646
  95.6 3.9 %collective-permute-done.19.fresh_ref = bf16[128,256]{1,0:T(8,128)(2,1)S(1)} collective-permute-done((bf16[128,256]{1,0:T(8,128)(2,1)S(1)}, bf16[128,256]{1,0:T(8,128)(2,1)S(1)}, u32[]{:S(2)}, u32[]{:S(2)}) %collective-permute-start.19) | collective-permute-done | bytes 65568 | tf_op jit(solution)/shard_map/ppermute | solution.py:646
  103.0 10.5 %attend.1 = (bf16[128,256]{1,0:T(8,128)(2,1)S(1)}, bf16[128,256]{1,0:T(8,128)(2,1)S(1)}) custom-call(s32[4]{0:T(128)S(1)} %copy-done.4, bf16[256,256]{1,0:T(8,128)(2,1)S(1)} %copy-done.6, bf16[16,2,128,128]{3,2,1,0:T(8,128)(2,1)S(1)} %all-to-all-done.near_keys, bf16[16,2,128,128]{3,2,1,0:T(8,128)(2,1)S(1)} %collective-permute-done.16.far_keys, ...), custom_call_target="tpu_custom_call" | custom-call | flops 4294967296 | bytes 5242880 | tf_op jit(solution)/shard_map/attend/pallas_call | solution.py:396
  115.0 3.7 %shard_map.144 = (bf16[4,272,256]{2,1,0:T(8,128)(2,1)S(1)}, bf16[4,272,256]{2,1,0:T(8,128)(2,1)S(1)}, bf16[4,272,256]{2,1,0:T(8,128)(2,1)S(1)}, bf16[4,272,256]{2,1,0:T(8,128)(2,1)S(1)}) custom-call(s32[4]{0:T(128)S(1)} %copy-done.5, bf16[128,256]{1,0:T(8,128)(2,1)S(1)} %get-tuple-element.46.near_ref, bf16[128,256]{1,0:T(8,128)(2,1)S(1)} %collective-permute-done.21.far_ref, ...), custom_call_target="tpu_custom_call" | custom-call | flops 1073741824 | bytes 4456448 | tf_op jit(solution)/shard_map/pallas_call | solution.py:44
  118.6 2.8 %collective-permute-start.23 = (bf16[4,272,256]{2,1,0:T(8,128)(2,1)S(1)}, bf16[4,272,256]{2,1,0:T(8,128)(2,1)S(1)}, u32[]{:S(2)}, u32[]{:S(2)}) collective-permute-start(bf16[4,272,256]{2,1,0:T(8,128)(2,1)S(1)} %get-tuple-element.51), channel_id=1, source_target_pairs={{0,2},{1,9},{2,4},{3,11},{4,6},{5,13},{6,0},{7,15},{8,10},{9,17},{... | collective-permute-start | bytes 1671176 | tf_op jit(solution)/shard_map/ppermute | solution.py:557
  121.4 3.8 %collective-permute-start.24 = (bf16[4,272,256]{2,1,0:T(8,128)(2,1)S(1)}, bf16[4,272,256]{2,1,0:T(8,128)(2,1)S(1)}, u32[]{:S(2)}, u32[]{:S(2)}) collective-permute-start(bf16[4,272,256]{2,1,0:T(8,128)(2,1)S(1)} %get-tuple-element.52), channel_id=1, source_target_pairs={{0,4},{1,17},{2,6},{3,19},{4,0},{5,21},{6,2},{7,23},{8,12},{9,25},... | collective-permute-start | bytes 1671176 | tf_op jit(solution)/shard_map/ppermute | solution.py:557
  125.2 5.7 %collective-permute-done.23.refs_1_ = bf16[4,272,256]{2,1,0:T(8,128)(2,1)S(1)} collective-permute-done((bf16[4,272,256]{2,1,0:T(8,128)(2,1)S(1)}, bf16[4,272,256]{2,1,0:T(8,128)(2,1)S(1)}, u32[]{:S(2)}, u32[]{:S(2)}) %collective-permute-start.23) | collective-permute-done | bytes 557088 | tf_op jit(solution)/shard_map/ppermute | solution.py:557
  131.0 7.2 %collective-permute-done.24.refs_2_ = bf16[4,272,256]{2,1,0:T(8,128)(2,1)S(1)} collective-permute-done((bf16[4,272,256]{2,1,0:T(8,128)(2,1)S(1)}, bf16[4,272,256]{2,1,0:T(8,128)(2,1)S(1)}, u32[]{:S(2)}, u32[]{:S(2)}) %collective-permute-start.24) | collective-permute-done | bytes 557088 | tf_op jit(solution)/shard_map/ppermute | solution.py:557
  138.5 2.5 %collective-permute-start.27 = (bf16[272,256]{1,0:T(8,128)(2,1)S(1)}, bf16[272,256]{1,0:T(8,128)(2,1)S(1)}, u32[]{:S(2)}, u32[]{:S(2)}) collective-permute-start(bf16[272,256]{1,0:T(8,128)(2,1)S(1)} %get-tuple-element.56), channel_id=1, source_target_pairs={{0,16},{1,5},{2,18},{3,7},{4,20},{5,1},{6,22},{7,3},{8,24},{9,13},... | collective-permute-start | bytes 417800 | tf_op jit(solution)/shard_map/ppermute | solution.py:557
  141.5 3.6 %collective-permute-done.26.refs_1_ = bf16[272,256]{1,0:T(8,128)(2,1)S(1)} collective-permute-done((bf16[272,256]{1,0:T(8,128)(2,1)S(1)}, bf16[272,256]{1,0:T(8,128)(2,1)S(1)}, u32[]{:S(2)}, u32[]{:S(2)}) %collective-permute-start.26) | collective-permute-done | bytes 139296 | tf_op jit(solution)/shard_map/ppermute | solution.py:557
  146.3 3.4 %collective-permute-start.29 = (bf16[144,256]{1,0:T(8,128)(2,1)S(1)}, bf16[144,256]{1,0:T(8,128)(2,1)S(1)}, u32[]{:S(2)}, u32[]{:S(2)}) collective-permute-start(bf16[144,256]{1,0:T(8,128)(2,1)S(1)} %get-tuple-element.59), channel_id=1, source_target_pairs={{0,1},{1,0},{2,3},{3,2},{4,5},{5,4},{6,7},{7,6},{8,9},{9,8},{10,11... | collective-permute-start | bytes 221192 | tf_op jit(solution)/shard_map/ppermute | solution.py:575
  152.3 5.2 %place.1 = bf16[2,3,128,1024]{3,2,1,0:T(8,128)(2,1)} custom-call(s32[3]{0:T(128)} %label_ref.1, bf16[16,2,128,1024]{3,2,1,0:T(8,128)(2,1)} %all-gather.2.cloned.1.call-done.in_ref), custom_call_target="tpu_custom_call" | custom-call | flops 4194304 | bytes 3145728 | tf_op jit(solution)/shard_map/place/pallas_call | solution.py:177
  (92 shorter events, 26.9 us)
Async XLA Ops:
  7.2 145.2 %all-gather.2.cloned.1.call-start = ((), (), s32[]{:S(2)}) async-start(), calls=%async_computation.2 | async-start | bytes 9437184 | tf_op jit(solution)/shard_map/all_gather | solution.py:596
  10.3 104.6 %collective-permute-start.22 = (bf16[256,8192]{1,0:T(8,128)(2,1)}, bf16[256,8192]{1,0:T(8,128)(2,1)}, u32[]{:S(2)}, u32[]{:S(2)}) collective-permute-start(bf16[256,8192]{1,0:T(8,128)(2,1)} %wo_ref.1), channel_id=1, source_target_pairs={{0,1},{1,0},{2,3},{3,2},{4,5},{5,4},{6,7},{7,6},{8,9},{9,8},{10,11... | collective-permute-start | bytes 12582920 | tf_op jit(solution)/shard_map/ppermute | solution.py:575
  13.6 33.9 %all-to-all-start = ((bf16[16,2,128,128]{3,2,1,0:T(8,128)(2,1)}), bf16[16,2,128,128]{3,2,1,0:T(8,128)(2,1)S(1)}, u32[]{:S(2)}, u32[]{:S(2)}) async-start(bf16[16,2,128,128]{3,2,1,0:T(8,128)(2,1)} %get-tuple-element.41), calls=%async_computation | async-start | bytes 2097152 | tf_op jit(solution)/shard_map/all_to_all | solution.py:570
  19.9 8.1 %collective-permute-start = (bf16[16,256]{1,0:T(8,128)(2,1)S(1)}, bf16[16,256]{1,0:T(8,128)(2,1)S(1)}, u32[]{:S(2)}, u32[]{:S(2)}) collective-permute-start(bf16[16,256]{1,0:T(8,128)(2,1)S(1)} %maximum_maximum_fusion.extra_ref), channel_id=1, source_target_pairs={{0,1},{1,0},{2,3},{3,2},{4,5},{5,4},{6,7},{7,6},{8,9},{9,8},{10,11... | collective-permute-start | bytes 24584 | tf_op jit(solution)/shard_map/ppermute | solution.py:575
  20.7 13.6 %collective-permute-start.2 = (bf16[2,32,256]{2,1,0:T(8,128)(2,1)S(1)}, bf16[2,32,256]{2,1,0:T(8,128)(2,1)S(1)}, u32[]{:S(2)}, u32[]{:S(2)}) collective-permute-start(bf16[2,32,256]{2,1,0:T(8,128)(2,1)S(1)} %get-tuple-element.36), channel_id=1, source_target_pairs={{0,32},{1,225},{32,64},{33,1},{64,96},{65,33},{96,128},{97,65},{12... | collective-permute-start | bytes 98312 | tf_op jit(solution)/shard_map/ppermute | solution.py:566
  26.3 8.0 %collective-permute-start.3 = (bf16[2,32,256]{2,1,0:T(8,128)(2,1)S(1)}, bf16[2,32,256]{2,1,0:T(8,128)(2,1)S(1)}, u32[]{:S(2)}, u32[]{:S(2)}) collective-permute-start(bf16[2,32,256]{2,1,0:T(8,128)(2,1)S(1)} %get-tuple-element.37), channel_id=1, source_target_pairs={{0,64},{1,193},{32,96},{33,225},{64,128},{65,1},{96,160},{97,33},{... | collective-permute-start | bytes 98312 | tf_op jit(solution)/shard_map/ppermute | solution.py:566
  27.5 6.9 %collective-permute-start.4 = (bf16[2,32,256]{2,1,0:T(8,128)(2,1)S(1)}, bf16[2,32,256]{2,1,0:T(8,128)(2,1)S(1)}, u32[]{:S(2)}, u32[]{:S(2)}) collective-permute-start(bf16[2,32,256]{2,1,0:T(8,128)(2,1)S(1)} %get-tuple-element.38), channel_id=1, source_target_pairs={{0,96},{1,161},{32,128},{33,193},{64,160},{65,225},{96,192},{97,1}... | collective-permute-start | bytes 98312 | tf_op jit(solution)/shard_map/ppermute | solution.py:566
  28.0 9.7 %collective-permute-start.5 = (bf16[2,32,256]{2,1,0:T(8,128)(2,1)S(1)}, bf16[2,32,256]{2,1,0:T(8,128)(2,1)S(1)}, u32[]{:S(2)}, u32[]{:S(2)}) collective-permute-start(bf16[2,32,256]{2,1,0:T(8,128)(2,1)S(1)} %get-tuple-element.39), channel_id=1, source_target_pairs={{0,0},{1,129},{32,32},{33,161},{64,64},{65,193},{96,96},{97,225},{... | collective-permute-start | bytes 98312 | tf_op jit(solution)/shard_map/ppermute | solution.py:566
  37.7 5.8 %collective-permute-start.6 = (bf16[2,144,256]{2,1,0:T(8,128)(2,1)S(1)}, bf16[2,144,256]{2,1,0:T(8,128)(2,1)S(1)}, u32[]{:S(2)}, u32[]{:S(2)}) collective-permute-start(bf16[2,144,256]{2,1,0:T(8,128)(2,1)S(1)} %shard_map.142), channel_id=1, source_target_pairs={{0,2},{1,9},{2,4},{3,11},{4,6},{5,13},{6,0},{7,15},{8,10},{9,17},{... | collective-permute-start | bytes 442376 | tf_op jit(solution)/shard_map/ppermute | solution.py:557
  39.4 6.6 %collective-permute-start.7 = (bf16[2,144,256]{2,1,0:T(8,128)(2,1)S(1)}, bf16[2,144,256]{2,1,0:T(8,128)(2,1)S(1)}, u32[]{:S(2)}, u32[]{:S(2)}) collective-permute-start(bf16[2,144,256]{2,1,0:T(8,128)(2,1)S(1)} %shard_map.142), channel_id=1, source_target_pairs={{0,4},{1,17},{2,6},{3,19},{4,0},{5,21},{6,2},{7,23},{8,12},{9,25},... | collective-permute-start | bytes 442376 | tf_op jit(solution)/shard_map/ppermute | solution.py:557
  46.2 11.1 %collective-permute-start.9 = (bf16[4,2,144,256]{3,2,1,0:T(8,128)(2,1)S(1)}, bf16[4,2,144,256]{3,2,1,0:T(8,128)(2,1)}, u32[]{:S(2)}, u32[]{:S(2)}) collective-permute-start(bf16[4,2,144,256]{3,2,1,0:T(8,128)(2,1)S(1)} %pad_maximum_fusion.refs_0_), channel_id=1, source_target_pairs={{0,8},{1,3},{2,10},{3,5},{4,12},{5,7},{6,14},{7,1},{8,16},{9,11},{... | collective-permute-start | bytes 1769480 | tf_op jit(solution)/shard_map/ppermute | solution.py:557
  47.5 33.3 %all-to-all-start.1 = ((bf16[16,2,128,128]{3,2,1,0:T(8,128)(2,1)}), bf16[16,2,128,128]{3,2,1,0:T(8,128)(2,1)S(1)}, u32[]{:S(2)}, u32[]{:S(2)}) async-start(bf16[16,2,128,128]{3,2,1,0:T(8,128)(2,1)} %get-tuple-element.42), calls=%async_computation.1 | async-start | bytes 2097152 | tf_op jit(solution)/shard_map/all_to_all | solution.py:570
  53.5 22.2 %collective-permute-start.10 = (bf16[4,2,144,256]{3,2,1,0:T(8,128)(2,1)S(1)}, bf16[4,2,144,256]{3,2,1,0:T(8,128)(2,1)}, u32[]{:S(2)}, u32[]{:S(2)}) collective-permute-start(bf16[4,2,144,256]{3,2,1,0:T(8,128)(2,1)S(1)} %pad_maximum_fusion.refs_0_), channel_id=1, source_target_pairs={{0,16},{1,5},{2,18},{3,7},{4,20},{5,1},{6,22},{7,3},{8,24},{9,13},... | collective-permute-start | bytes 1769480 | tf_op jit(solution)/shard_map/ppermute | solution.py:557
  56.4 23.1 %collective-permute-start.11 = (bf16[4,2,144,256]{3,2,1,0:T(8,128)(2,1)S(1)}, bf16[4,2,144,256]{3,2,1,0:T(8,128)(2,1)}, u32[]{:S(2)}, u32[]{:S(2)}) collective-permute-start(bf16[4,2,144,256]{3,2,1,0:T(8,128)(2,1)S(1)} %pad_maximum_fusion.refs_0_), channel_id=1, source_target_pairs={{0,24},{1,7},{2,26},{3,1},{4,28},{5,3},{6,30},{7,5},{8,0},{9,15},{... | collective-permute-start | bytes 1769480 | tf_op jit(solution)/shard_map/ppermute | solution.py:557
  57.3 22.5 %collective-permute-start.12 = (bf16[4,2,144,256]{3,2,1,0:T(8,128)(2,1)S(1)}, bf16[4,2,144,256]{3,2,1,0:T(8,128)(2,1)S(1)}, u32[]{:S(2)}, u32[]{:S(2)}) collective-permute-start(bf16[4,2,144,256]{3,2,1,0:T(8,128)(2,1)S(1)} %pad_maximum_fusion.refs_0_), channel_id=1, source_target_pairs={{0,1},{1,0},{2,3},{3,2},{4,5},{5,4},{6,7},{7,6},{8,9},{9,8},{10,11... | collective-permute-start | bytes 1769480 | tf_op jit(solution)/shard_map/ppermute | solution.py:575
  57.3 23.5 %collective-permute-start.13 = (bf16[4,2,144,256]{3,2,1,0:T(8,128)(2,1)}, bf16[4,2,144,256]{3,2,1,0:T(8,128)(2,1)}, u32[]{:S(2)}, u32[]{:S(2)}) collective-permute-start(bf16[4,2,144,256]{3,2,1,0:T(8,128)(2,1)} %collective-permute-done.9.refs_1_), channel_id=1, source_target_pairs={{0,1},{1,0},{2,3},{3,2},{4,5},{5,4},{6,7},{7,6},{8,9},{9,8},{10,11... | collective-permute-start | bytes 1769480 | tf_op jit(solution)/shard_map/ppermute | solution.py:575
  80.6 20.8 %collective-permute-start.16 = (bf16[16,2,128,128]{3,2,1,0:T(8,128)(2,1)S(1)}, bf16[16,2,128,128]{3,2,1,0:T(8,128)(2,1)S(1)}, u32[]{:S(2)}, u32[]{:S(2)}) collective-permute-start(bf16[16,2,128,128]{3,2,1,0:T(8,128)(2,1)S(1)} %all-to-all-done.near_keys), channel_id=1, source_target_pairs={{0,1},{1,0},{2,3},{3,2},{4,5},{5,4},{6,7},{7,6},{8,9},{9,8},{10,11... | collective-permute-start | bytes 3145736 | tf_op jit(solution)/shard_map/ppermute | solution.py:575
  80.8 20.6 %collective-permute-start.17 = (bf16[16,2,128,128]{3,2,1,0:T(8,128)(2,1)S(1)}, bf16[16,2,128,128]{3,2,1,0:T(8,128)(2,1)}, u32[]{:S(2)}, u32[]{:S(2)}) collective-permute-start(bf16[16,2,128,128]{3,2,1,0:T(8,128)(2,1)S(1)} %all-to-all-done.1.near_values), channel_id=1, source_target_pairs={{0,1},{1,0},{2,3},{3,2},{4,5},{5,4},{6,7},{7,6},{8,9},{9,8},{10,11... | collective-permute-start | bytes 3145736 | tf_op jit(solution)/shard_map/ppermute | solution.py:575
  92.4 7.1 %collective-permute-start.19 = (bf16[128,256]{1,0:T(8,128)(2,1)S(1)}, bf16[128,256]{1,0:T(8,128)(2,1)S(1)}, u32[]{:S(2)}, u32[]{:S(2)}) collective-permute-start(bf16[128,256]{1,0:T(8,128)(2,1)S(1)} %pad_maximum_fusion.1), channel_id=1, source_target_pairs={{0,0},{1,2},{16,1},{17,3},{2,4},{3,6},{18,5},{19,7},{4,8},{5,10},{... | collective-permute-start | bytes 196616 | tf_op jit(solution)/shard_map/ppermute | solution.py:646
  118.6 12.3 %collective-permute-start.23 = (bf16[4,272,256]{2,1,0:T(8,128)(2,1)S(1)}, bf16[4,272,256]{2,1,0:T(8,128)(2,1)S(1)}, u32[]{:S(2)}, u32[]{:S(2)}) collective-permute-start(bf16[4,272,256]{2,1,0:T(8,128)(2,1)S(1)} %get-tuple-element.51), channel_id=1, source_target_pairs={{0,2},{1,9},{2,4},{3,11},{4,6},{5,13},{6,0},{7,15},{8,10},{9,17},{... | collective-permute-start | bytes 1671176 | tf_op jit(solution)/shard_map/ppermute | solution.py:557
  121.4 16.7 %collective-permute-start.24 = (bf16[4,272,256]{2,1,0:T(8,128)(2,1)S(1)}, bf16[4,272,256]{2,1,0:T(8,128)(2,1)S(1)}, u32[]{:S(2)}, u32[]{:S(2)}) collective-permute-start(bf16[4,272,256]{2,1,0:T(8,128)(2,1)S(1)} %get-tuple-element.52), channel_id=1, source_target_pairs={{0,4},{1,17},{2,6},{3,19},{4,0},{5,21},{6,2},{7,23},{8,12},{9,25},... | collective-permute-start | bytes 1671176 | tf_op jit(solution)/shard_map/ppermute | solution.py:557
  125.2 12.9 %collective-permute-start.25 = (bf16[4,272,256]{2,1,0:T(8,128)(2,1)S(1)}, bf16[4,272,256]{2,1,0:T(8,128)(2,1)S(1)}, u32[]{:S(2)}, u32[]{:S(2)}) collective-permute-start(bf16[4,272,256]{2,1,0:T(8,128)(2,1)S(1)} %get-tuple-element.53), channel_id=1, source_target_pairs={{0,6},{1,25},{2,0},{3,27},{4,2},{5,29},{6,4},{7,31},{8,14},{9,1},{... | collective-permute-start | bytes 1671176 | tf_op jit(solution)/shard_map/ppermute | solution.py:557
  138.4 6.7 %collective-permute-start.26 = (bf16[272,256]{1,0:T(8,128)(2,1)S(1)}, bf16[272,256]{1,0:T(8,128)(2,1)S(1)}, u32[]{:S(2)}, u32[]{:S(2)}) collective-permute-start(bf16[272,256]{1,0:T(8,128)(2,1)S(1)} %get-tuple-element.55), channel_id=1, source_target_pairs={{0,8},{1,3},{2,10},{3,5},{4,12},{5,7},{6,14},{7,1},{8,16},{9,11},{... | collective-permute-start | bytes 417800 | tf_op jit(solution)/shard_map/ppermute | solution.py:557
  138.5 6.6 %collective-permute-start.27 = (bf16[272,256]{1,0:T(8,128)(2,1)S(1)}, bf16[272,256]{1,0:T(8,128)(2,1)S(1)}, u32[]{:S(2)}, u32[]{:S(2)}) collective-permute-start(bf16[272,256]{1,0:T(8,128)(2,1)S(1)} %get-tuple-element.56), channel_id=1, source_target_pairs={{0,16},{1,5},{2,18},{3,7},{4,20},{5,1},{6,22},{7,3},{8,24},{9,13},... | collective-permute-start | bytes 417800 | tf_op jit(solution)/shard_map/ppermute | solution.py:557
  (23 other events, 252.2 us)
Sparse Core Ops, SparseCore 0:
  10.4 99.7 all-gather.1
